TPU v7x, 32 devices: a whole 2x2x4 slice. The times are simulated.
32 devices in a mesh: grow: 16 (over z, y, core), trans: 2 (over x).
Axes of the slice: x: 2, y: 2, z: 4, core: 2. Of those that a mesh axis runs over, the one named last changes fastest.
Arguments:
- phase_label: int32 [384, 16, 128], P('grow', 'trans'), may hold values from 0 to 3
- grain_label: int32 [384, 16, 128], P('grow', 'trans'), may hold values from 0 to 31
- grain_orient: int32 [32], replicated, may hold values from 0 to 7
- orient_mobility: float32 [8], replicated, may hold values from 0.4 to 1.2
- solute_init: float32 [2, 384, 16, 128], P(None, 'grow', 'trans'), may hold values from 0.1 to 0.5
- partition: float32 [4, 2], replicated, may hold values from -0.5 to 0.5
Outputs:
- phase_out: float32 [4, 384, 16, 128], P(None, 'grow', 'trans')
- solute_out: float32 [2, 384, 16, 128], P(None, 'grow', 'trans')
All inputs are finite; a program needn't handle non-finite values.
Results may differ from a plain program's by a relative error of at most 0.00002.
Values sent between devices are 32-bit elements; how exact they have to be, the bound alone decides.
No kernel may reach another device: no remote copies, remote signals or barrier semaphores. Data moves between devices by JAX's collectives and lax.ppermute only.
A program may use at most 64 MiB of HBM per device.

v0:
```python
import jax
import jax.numpy as jnp
from jax import lax
from jax.sharding import PartitionSpec as P

SHIFT = 16


ANISOTROPY = 1.5
WELL_HEIGHT = 4.0
TIME_STEP = 0.06
LIQUID_DIFFUSION = 1.0
SOLID_DIFFUSION = 0.1
COOLING_WEIGHTS = (-1.0, 0.8, 0.7, 0.6)
FIRST_WEIGHTS = (0.5, -1.0, 0.4, 0.3)
SECOND_WEIGHTS = (0.4, 0.3, -1.0, 0.5)
INFLOW_FIRST = 0.3
INFLOW_SECOND = 0.2
LIQUID_MOBILITY = 1.0


def padded_2(cells, sides, width):
    for axis, dim in sides:
        count = lax.axis_size(axis)
        head = lax.slice_in_dim(cells, 0, width, axis=dim)
        tail = lax.slice_in_dim(cells, cells.shape[dim] - width, cells.shape[dim], axis=dim)
        cells = jnp.concatenate(
            [
                lax.ppermute(tail, axis, [(i, (i + 1) % count) for i in range(count)]),
                cells,
                lax.ppermute(head, axis, [((i + 1) % count, i) for i in range(count)]),
            ],
            axis=dim,
        )
    return cells


def from_behind(value, axis, steps):
    count = lax.axis_size(axis)
    initial, last = (max(0, -steps), min(count, count - steps))
    return lax.ppermute(value, axis, [(source, source + steps) for source in range(initial, last)])


def advance(padded, mobility, undercool, partition):
    centre = padded[:, 1:-1, 1:-1]
    plane_up = padded[:, 2:, 1:-1]
    plane_down = padded[:, :-2, 1:-1]
    row_next = padded[:, 1:-1, 2:]
    row_prev = padded[:, 1:-1, :-2]
    col_next = jnp.roll(centre, -1, axis=3)
    col_prev = jnp.roll(centre, 1, axis=3)
    phases = centre[:4]
    solutes = centre[4:]
    laplace = ANISOTROPY * (plane_up[:4] + plane_down[:4] - 2.0 * phases)
    laplace = laplace + (row_next[:4] + row_prev[:4] - 2.0 * phases)
    laplace = laplace + (col_next[:4] + col_prev[:4] - 2.0 * phases)
    cooling_w = jnp.array(COOLING_WEIGHTS, dtype=phases.dtype).reshape(4, 1, 1, 1)
    first_w = jnp.array(FIRST_WEIGHTS, dtype=phases.dtype).reshape(4, 1, 1, 1)
    second_w = jnp.array(SECOND_WEIGHTS, dtype=phases.dtype).reshape(4, 1, 1, 1)
    driving = cooling_w * undercool[None] + first_w * solutes[0][None] + second_w * solutes[1][None]
    forcing = laplace + WELL_HEIGHT * phases * (1.0 - phases) * (phases - 0.5 + driving)
    growth_rate = mobility[None] * (forcing - jnp.mean(forcing, axis=0, keepdims=True))
    trials = jnp.clip(phases + TIME_STEP * growth_rate, 0.0, 1.0)
    new_phases = trials / jnp.sum(trials, axis=0, keepdims=True)
    own_diffusion = SOLID_DIFFUSION + (LIQUID_DIFFUSION - SOLID_DIFFUSION) * centre[0]
    influx = jnp.zeros_like(solutes)
    for neighbour in (plane_up, plane_down, row_next, row_prev, col_next, col_prev):
        other = SOLID_DIFFUSION + (LIQUID_DIFFUSION - SOLID_DIFFUSION) * neighbour[0]
        influx = influx + 0.5 * (other + own_diffusion)[None] * (neighbour[4:] - solutes)
    changes = new_phases - phases
    rejected = partition[0][:, None, None, None] * changes[0][None]
    rejected = rejected + partition[1][:, None, None, None] * changes[1][None]
    rejected = rejected + partition[2][:, None, None, None] * changes[2][None]
    rejected = rejected + partition[3][:, None, None, None] * changes[3][None]
    new_solutes = solutes + TIME_STEP * influx - rejected
    return jnp.concatenate([new_phases, new_solutes], axis=0)


def fix_ends(padded, margin, first_slab, last_slab):
    lower_edge = padded[:, margin : margin + 1]
    upper_edge = padded[:, -margin - 1 : -margin]
    lower_ghost = jnp.where(first_slab, lower_edge, padded[:, :margin])
    upper_ghost = jnp.where(last_slab, upper_edge, padded[:, -margin:])
    return jnp.concatenate([lower_ghost, padded[:, margin:-margin], upper_ghost], axis=1)


def cooling(heights, total_depth):
    return (2.0 * (0.5 - (heights + 0.5) / total_depth))[:, None, None]


def side_rims(fields):
    return padded_2(fields, (("trans", 2),), 1)


def window_step(window, base, total_depth, last_slab, partition):
    length = window.shape[1]
    offsets = jnp.arange(length, dtype=jnp.int32)
    top_offset = jnp.clip(total_depth - 1 - base, 0, length - 1)
    edge = lax.dynamic_slice_in_dim(window, top_offset, 1, 1)
    beyond = jnp.logical_and(last_slab, offsets > top_offset)[None, :, None, None]
    window = jnp.where(beyond, edge, window)
    padded = side_rims(window[:6])
    heights = (base + 1 + jnp.arange(length - 2, dtype=jnp.int32)).astype(window.dtype)
    stepped = advance(padded, window[6, 1:-1], cooling(heights, total_depth), partition)
    return jnp.concatenate([stepped, window[6:, 1:-1]], axis=0)


def final_step(window, undercool, partition):
    padded = side_rims(window[:6])
    return advance(padded, window[6, 1:-1], undercool, partition)


def shards(phase_label, grain_label, grain_orient, orient_mobility, solute_init, partition):
    slab_index = lax.axis_index("grow")
    slab_count = lax.axis_size("grow")
    planes = phase_label.shape[0]
    first_slab = slab_index == 0
    last_slab = slab_index == slab_count - 1
    orients = orient_mobility.shape[0]
    grains = grain_orient.shape[0]
    orient_ids = jnp.arange(orients, dtype=jnp.int32)
    grain_mobility = jnp.sum(
        jnp.where(grain_orient[:, None] == orient_ids[None, :], orient_mobility[None, :], 0.0),
        axis=1,
    )
    grain_ids = jnp.arange(grains, dtype=jnp.int32)[:, None, None, None]
    mobility = jnp.sum(
        jnp.where(grain_label[None] == grain_ids, grain_mobility[:, None, None, None], 0.0), axis=0
    )
    labels = jnp.arange(4, dtype=jnp.int32)[:, None, None, None]
    phases = (phase_label[None] == labels).astype(solute_init.dtype)
    fields = jnp.concatenate([phases, solute_init], axis=0)
    total_depth = planes * slab_count
    heights = (slab_index * planes + jnp.arange(planes, dtype=jnp.int32)).astype(fields.dtype)
    undercool = cooling(heights, total_depth)
    inflow = jnp.array(
        [1.0, 0.0, 0.0, 0.0, INFLOW_FIRST, INFLOW_SECOND, LIQUID_MOBILITY], dtype=fields.dtype
    )
    stacked = jnp.concatenate([fields, mobility[None]], axis=0)
    received = from_behind(stacked[:, : SHIFT + 3], "grow", -1)
    window = jnp.concatenate([stacked[:, SHIFT - 3 :], received], axis=1)
    base = slab_index * planes + SHIFT - 3
    for turn in range(2):
        window = window_step(window, base + turn, total_depth, last_slab, partition)
    new_index = slab_index * planes - 1 + jnp.arange(window.shape[1], dtype=jnp.int32)
    liquid_mask = (new_index >= total_depth - SHIFT)[None, :, None, None]
    window = jnp.where(liquid_mask, inflow[:, None, None, None], window)
    window = fix_ends(window, 1, first_slab, last_slab)
    fields = final_step(window, undercool, partition)
    return (fields[:4], fields[4:])


def solution(mesh):
    placed = (
        P("grow", "trans", None),
        P("grow", "trans", None),
        P(),
        P(),
        P(None, "grow", "trans", None),
        P(),
    )
    return jax.shard_map(
        shards,
        mesh=mesh,
        in_specs=placed,
        out_specs=(P(None, "grow", "trans", None), P(None, "grow", "trans", None)),
        check_vma=False,
    )
```

profile of v0, /device:TPU:4, one launch (start us, length us, event | category | flops | bytes accessed | tf_op | source)
XLA Modules:
  0.0 44.3 jit_solution(15175029182013779503)
XLA Ops:
  0.6 0.9 %fusion.34 = f32[4,24,8,128]{3,2,1,0:T(8,128)S(1)} fusion(s32[24,8,128]{2,1,0:T(8,128)} %param.16), kind=kLoop, calls=%fused_computation.87 | loop fusion | flops 196608 | bytes 491520 | tf_op jit(solution)/shard_map/convert_element_type | solution.py:131
  1.6 0.0 copy-start.4
  1.6 0.8 %select_reduce_fusion.1 = f32[32]{0:T(128)S(1)} fusion(f32[8]{0:T(128)} %param.19, s32[32]{0:T(128)} %param.18), kind=kLoop, calls=%fused_computation.299 | loop fusion | flops 736 | bytes 288 | tf_op jit(solution)/shard_map/reduce_sum | solution.py:122
  2.4 1.3 %select_reduce_fusion = f32[24,8,128]{2,1,0:T(8,128)S(1)} fusion(f32[32]{0:T(128)S(1)} %select_reduce_fusion.1, s32[24,8,128]{2,1,0:T(8,128)} %param.17), kind=kLoop, calls=%fused_computation | loop fusion | flops 2334720 | bytes 196736 | tf_op jit(solution)/shard_map/reduce_sum | solution.py:127
  3.7 1.0 %pad_maximum_fusion.4 = f32[7,19,8,128]{3,2,1,0:T(8,128)S(1)} fusion(f32[1,24,8,128]{3,2,1,0:T(8,128)S(1)} %bitcast.83, f32[2,24,8,128]{3,2,1,0:T(8,128)} %param.20, f32[4,24,8,128]{3,2,1,0:T(8,128)S(1)} %fusion.34), kind=kLoop, calls=%fused_computation.40 | loop fusion | flops 272384 | bytes 1232896 | tf_op jit(solution)/shard_map/concatenate | solution.py:139
  4.6 1.9 %collective-permute-start = (f32[7,19,8,128]{3,2,1,0:T(8,128)S(1)}, f32[7,19,8,128]{3,2,1,0:T(8,128)S(1)}, u32[]{:S(2)}, u32[]{:S(2)}) collective-permute-start(f32[7,19,8,128]{3,2,1,0:T(8,128)S(1)} %pad_maximum_fusion.4), channel_id=1, source_target_pairs={{2,0},{4,2},{6,4},{8,6},{10,8},{12,10},{14,12},{16,14},{18,16},{20... | collective-permute-start | bytes 1634312 | tf_op jit(solution)/shard_map/ppermute | solution.py:41
  6.6 0.2 slice_reduce_fusion.3
  6.9 0.1 broadcast_multiply_fusion.5
  7.0 0.1 broadcast_multiply_fusion.4
  7.0 0.1 broadcast_multiply_fusion.3
  7.1 6.3 %collective-permute-done = f32[7,19,8,128]{3,2,1,0:T(8,128)S(1)} collective-permute-done((f32[7,19,8,128]{3,2,1,0:T(8,128)S(1)}, f32[7,19,8,128]{3,2,1,0:T(8,128)S(1)}, u32[]{:S(2)}, u32[]{:S(2)}) %collective-permute-start) | collective-permute-done | bytes 544800 | tf_op jit(solution)/shard_map/ppermute | solution.py:41
  13.5 0.1 fusion
  13.5 0.1 broadcast_select_fusion
  13.7 0.2 fusion.192
  13.9 0.1 fusion.191
  14.1 1.6 %collective-permute-start.1 = (f32[6,30,1,128]{3,1,2,0:T(8,128)S(1)}, f32[6,30,1,128]{3,1,2,0:T(8,128)S(1)}, u32[]{:S(2)}, u32[]{:S(2)}) collective-permute-start(f32[6,30,1,128]{3,1,2,0:T(8,128)S(1)} %copy.34), channel_id=1, source_target_pairs={{1,0},{0,1},{3,2},{2,3},{5,4},{4,5},{7,6},{6,7},{9,8},{8,9},{11,10... | collective-permute-start | bytes 276488 | tf_op jit(solution)/shard_map/ppermute | solution.py:31
  15.6 0.6 %collective-permute-start.2 = (f32[6,30,1,128]{3,1,2,0:T(8,128)S(1)}, f32[6,30,1,128]{3,1,2,0:T(8,128)S(1)}, u32[]{:S(2)}, u32[]{:S(2)}) collective-permute-start(f32[6,30,1,128]{3,1,2,0:T(8,128)S(1)} %copy.36), channel_id=1, source_target_pairs={{0,1},{1,0},{2,3},{3,2},{4,5},{5,4},{6,7},{7,6},{8,9},{9,8},{10,11... | collective-permute-start | bytes 276488 | tf_op jit(solution)/shard_map/ppermute | solution.py:29
  16.2 0.2 fusion.193
  16.5 2.2 %collective-permute-done.1 = f32[6,30,1,128]{3,1,2,0:T(8,128)S(1)} collective-permute-done((f32[6,30,1,128]{3,1,2,0:T(8,128)S(1)}, f32[6,30,1,128]{3,1,2,0:T(8,128)S(1)}, u32[]{:S(2)}, u32[]{:S(2)}) %collective-permute-start.1) | collective-permute-done | bytes 92192 | tf_op jit(solution)/shard_map/ppermute | solution.py:31
  18.7 0.1 copy.35
  18.8 2.4 %collective-permute-done.2 = f32[6,30,1,128]{3,1,2,0:T(8,128)S(1)} collective-permute-done((f32[6,30,1,128]{3,1,2,0:T(8,128)S(1)}, f32[6,30,1,128]{3,1,2,0:T(8,128)S(1)}, u32[]{:S(2)}, u32[]{:S(2)}) %collective-permute-start.2) | collective-permute-done | bytes 92192 | tf_op jit(solution)/shard_map/ppermute | solution.py:29
  21.3 0.1 copy.37
  21.4 0.0 copy-start.2
  21.4 0.0 copy-start.3
  21.4 0.2 fusion.119
  21.6 0.5 %copy-done.2 = f32[4]{0:T(128)S(1)} copy-done((f32[4]{0:T(128)S(1)}, f32[4]{0:T(128)}, u32[]{:S(2)}) %copy-start.2) | copy-done | bytes 40
  22.0 0.0 copy-done.3
  22.0 0.7 %fusion.189 = (f32[28,8,128]{2,1,0:T(8,128)S(1)}, f32[4,28,8,128]{3,2,1,0:T(8,128)S(1)}) fusion(f32[28,8,128]{2,1,0:T(8,128)S(1)} %get-tuple-element.35, f32[4]{0:T(128)S(1)} %copy-done.3, f32[28,8,128]{2,1,0:T(8,128)S(1)} %get-tuple-element.36, f32[4]{0:T(128)S(1)} %copy-done.2, f32[4,28]{1,0:T(4,128)S(1)} %broadcast_multiply_fusion.5, ...), kind=kLoop, calls=%fused_computation.321 | loop fusion | flops 2953216 | bytes 4477408 | tf_op jit(solution)/shard_map/reduce_sum | solution.py:62
  22.7 0.1 fusion.184
  22.8 0.1 slice_subtract_fusion
  23.0 0.4 fusion.40
  23.4 0.1 pad_maximum_fusion.2
  23.5 0.1 broadcast_select_fusion.1
  23.6 0.2 fusion.195
  23.9 0.1 fusion.194
  24.0 0.5 %collective-permute-start.3 = (f32[6,28,1,128]{3,1,2,0:T(8,128)S(1)}, f32[6,28,1,128]{3,1,2,0:T(8,128)S(1)}, u32[]{:S(2)}, u32[]{:S(2)}) collective-permute-start(f32[6,28,1,128]{3,1,2,0:T(8,128)S(1)} %copy.38), channel_id=1, source_target_pairs={{1,0},{0,1},{3,2},{2,3},{5,4},{4,5},{7,6},{6,7},{9,8},{8,9},{11,10... | collective-permute-start | bytes 258056 | tf_op jit(solution)/shard_map/ppermute | solution.py:31
  24.5 1.6 %collective-permute-start.4 = (f32[6,28,1,128]{3,1,2,0:T(8,128)S(1)}, f32[6,28,1,128]{3,1,2,0:T(8,128)S(1)}, u32[]{:S(2)}, u32[]{:S(2)}) collective-permute-start(f32[6,28,1,128]{3,1,2,0:T(8,128)S(1)} %copy.40), channel_id=1, source_target_pairs={{0,1},{1,0},{2,3},{3,2},{4,5},{5,4},{6,7},{7,6},{8,9},{9,8},{10,11... | collective-permute-start | bytes 258056 | tf_op jit(solution)/shard_map/ppermute | solution.py:29
  26.1 0.2 fusion.196
  26.4 3.3 %collective-permute-done.3 = f32[6,28,1,128]{3,1,2,0:T(8,128)S(1)} collective-permute-done((f32[6,28,1,128]{3,1,2,0:T(8,128)S(1)}, f32[6,28,1,128]{3,1,2,0:T(8,128)S(1)}, u32[]{:S(2)}, u32[]{:S(2)}) %collective-permute-start.3) | collective-permute-done | bytes 86048 | tf_op jit(solution)/shard_map/ppermute | solution.py:31
  29.7 0.1 copy.39
  29.8 2.0 %collective-permute-done.4 = f32[6,28,1,128]{3,1,2,0:T(8,128)S(1)} collective-permute-done((f32[6,28,1,128]{3,1,2,0:T(8,128)S(1)}, f32[6,28,1,128]{3,1,2,0:T(8,128)S(1)}, u32[]{:S(2)}, u32[]{:S(2)}) %collective-permute-start.4) | collective-permute-done | bytes 86048 | tf_op jit(solution)/shard_map/ppermute | solution.py:29
  31.8 0.1 copy.41
  31.9 0.2 fusion.148
  32.1 0.6 %fusion.187 = (f32[26,8,128]{2,1,0:T(8,128)S(1)}, f32[4,26,8,128]{3,2,1,0:T(8,128)S(1)}) fusion(f32[26,8,128]{2,1,0:T(8,128)S(1)} %get-tuple-element.50, f32[4]{0:T(128)S(1)} %copy-done.3, f32[26,8,128]{2,1,0:T(8,128)S(1)} %get-tuple-element.51, f32[4]{0:T(128)S(1)} %copy-done.2, f32[4,26]{1,0:T(4,128)S(1)} %broadcast_multiply_fusion.4, ...), kind=kLoop, calls=%fused_computation.320 | loop fusion | flops 2742272 | bytes 4161984 | tf_op jit(solution)/shard_map/reduce_sum | solution.py:62
  32.7 0.1 fusion.183
  32.8 0.1 slice_subtract_fusion.1
  33.0 0.0 copy-start.5
  33.0 0.3 fusion.58
  33.3 0.3 copy-done.5
  33.6 0.1 maximum_select_fusion
  33.9 0.2 fusion.197
  34.1 0.2 fusion.198
  34.3 0.1 pad_maximum_fusion.21
  34.5 0.1 collective-permute-start.5
  34.6 2.1 %collective-permute-start.6 = (f32[6,26,1,128]{3,1,2,0:T(8,128)S(1)}, f32[6,26,1,128]{3,1,2,0:T(8,128)S(1)}, u32[]{:S(2)}, u32[]{:S(2)}) collective-permute-start(f32[6,26,1,128]{3,1,2,0:T(8,128)S(1)} %copy.44), channel_id=1, source_target_pairs={{0,1},{1,0},{2,3},{3,2},{4,5},{5,4},{6,7},{7,6},{8,9},{9,8},{10,11... | collective-permute-start | bytes 239624 | tf_op jit(solution)/shard_map/ppermute | solution.py:29
  36.7 3.5 %collective-permute-done.5 = f32[6,26,1,128]{3,1,2,0:T(8,128)S(1)} collective-permute-done((f32[6,26,1,128]{3,1,2,0:T(8,128)S(1)}, f32[6,26,1,128]{3,1,2,0:T(8,128)S(1)}, u32[]{:S(2)}, u32[]{:S(2)}) %collective-permute-start.5) | collective-permute-done | bytes 79904 | tf_op jit(solution)/shard_map/ppermute | solution.py:31
  40.2 0.1 copy.43
  40.3 1.2 %collective-permute-done.6 = f32[6,26,1,128]{3,1,2,0:T(8,128)S(1)} collective-permute-done((f32[6,26,1,128]{3,1,2,0:T(8,128)S(1)}, f32[6,26,1,128]{3,1,2,0:T(8,128)S(1)}, u32[]{:S(2)}, u32[]{:S(2)}) %collective-permute-start.6) | collective-permute-done | bytes 79904 | tf_op jit(solution)/shard_map/ppermute | solution.py:29
  41.4 0.1 copy.45
  41.5 0.2 fusion.172
  41.7 0.6 %fusion.185 = (f32[24,8,128]{2,1,0:T(8,128)S(1)}, f32[4,24,8,128]{3,2,1,0:T(8,128)S(1)}) fusion(f32[24,8,128]{2,1,0:T(8,128)S(1)} %get-tuple-element.62, f32[4]{0:T(128)S(1)} %copy-done.3, f32[24,8,128]{2,1,0:T(8,128)S(1)} %get-tuple-element.64, f32[4]{0:T(128)S(1)} %copy-done.2, f32[4,24]{1,0:T(4,128)S(1)} %broadcast_multiply_fusion.3, ...), kind=kLoop, calls=%fused_computation.319 | loop fusion | flops 2727936 | bytes 3805600 | tf_op jit(solution)/shard_map/reduce_sum | solution.py:62
  42.3 0.1 fusion.182
  42.4 0.9 %slice_subtract_fusion.2 = (f32[4,24,8,128]{3,2,1,0:T(8,128)S(1)}, f32[4,24,8,128]{3,2,1,0:T(8,128)}) fusion(f32[7,26,8,128]{3,2,1,0:T(8,128)S(1)} %maximum_select_fusion, f32[24,8,128]{2,1,0:T(8,128)S(1)} %fusion.182, f32[4,24,8,128]{3,2,1,0:T(8,128)S(1)} %get-tuple-element.11, f32[24,8,128]{2,1,0:T(8,128)S(1)} %broadcast_multiply_fusion.2, ...), kind=kLoop, calls=%fused_computation.89 | loop fusion | flops 688128 | bytes 1867776 | tf_op jit(solution)/shard_map/sub | solution.py:70
  43.3 1.0 %fusion.76 = f32[2,24,8,128]{3,2,1,0:T(8,128)} fusion(f32[6,24,8,127]{3,2,1,0:T(8,128)S(1)} %get-tuple-element.70, f32[6,24,8,1]{3,2,1,0:T(8,128)S(1)} %get-tuple-element.72, f32[6,24,8,1]{3,2,1,0:T(8,128)S(1)} %get-tuple-element.71, f32[6,24,8,127]{3,2,1,0:T(8,128)S(1)} %get-tuple-element.69, f32[6,26,8,128]{3,2,1,0:T(8,128)S(1)} %slice.668, ...), kind=kLoop, calls=%fused_computation.146 | loop fusion | flops 1622016 | bytes 4100128 | tf_op jit(solution)/shard_map/sub | solution.py:75
  (34 shorter events, 0.5 us)
Async XLA Ops:
  0.6 6.0 %copy-start.1 = (f32[4,2]{0,1:T(2,128)S(1)}, f32[4,2]{0,1:T(2,128)}, u32[]{:S(2)}) copy-start(f32[4,2]{0,1:T(2,128)} %param.21) | copy-start | bytes 100
  1.6 5.3 %copy-start.4 = (f32[4]{0:T(128)S(1)}, f32[4]{0:T(128)}, u32[]{:S(2)}) copy-start(f32[4]{0:T(128)} %constant.53.clone) | copy-start | bytes 52
  1.6 11.9 %copy-start = (f32[2,24,8,128]{3,2,1,0:T(8,128)S(1)}, f32[2,24,8,128]{3,2,1,0:T(8,128)}, u32[]{:S(2)}) copy-start(f32[2,24,8,128]{3,2,1,0:T(8,128)} %param.20) | copy-start | bytes 589828
  4.6 8.8 %collective-permute-start = (f32[7,19,8,128]{3,2,1,0:T(8,128)S(1)}, f32[7,19,8,128]{3,2,1,0:T(8,128)S(1)}, u32[]{:S(2)}, u32[]{:S(2)}) collective-permute-start(f32[7,19,8,128]{3,2,1,0:T(8,128)S(1)} %pad_maximum_fusion.4), channel_id=1, source_target_pairs={{2,0},{4,2},{6,4},{8,6},{10,8},{12,10},{14,12},{16,14},{18,16},{20... | collective-permute-start | bytes 1634312 | tf_op jit(solution)/shard_map/ppermute | solution.py:41
  14.1 4.7 %collective-permute-start.1 = (f32[6,30,1,128]{3,1,2,0:T(8,128)S(1)}, f32[6,30,1,128]{3,1,2,0:T(8,128)S(1)}, u32[]{:S(2)}, u32[]{:S(2)}) collective-permute-start(f32[6,30,1,128]{3,1,2,0:T(8,128)S(1)} %copy.34), channel_id=1, source_target_pairs={{1,0},{0,1},{3,2},{2,3},{5,4},{4,5},{7,6},{6,7},{9,8},{8,9},{11,10... | collective-permute-start | bytes 276488 | tf_op jit(solution)/shard_map/ppermute | solution.py:31
  15.6 5.6 %collective-permute-start.2 = (f32[6,30,1,128]{3,1,2,0:T(8,128)S(1)}, f32[6,30,1,128]{3,1,2,0:T(8,128)S(1)}, u32[]{:S(2)}, u32[]{:S(2)}) collective-permute-start(f32[6,30,1,128]{3,1,2,0:T(8,128)S(1)} %copy.36), channel_id=1, source_target_pairs={{0,1},{1,0},{2,3},{3,2},{4,5},{5,4},{6,7},{7,6},{8,9},{9,8},{10,11... | collective-permute-start | bytes 276488 | tf_op jit(solution)/shard_map/ppermute | solution.py:29
  21.4 0.7 %copy-start.2 = (f32[4]{0:T(128)S(1)}, f32[4]{0:T(128)}, u32[]{:S(2)}) copy-start(f32[4]{0:T(128)} %constant.54.clone) | copy-start | bytes 52
  21.4 0.7 %copy-start.3 = (f32[4]{0:T(128)S(1)}, f32[4]{0:T(128)}, u32[]{:S(2)}) copy-start(f32[4]{0:T(128)} %constant.55.clone) | copy-start | bytes 52
  24.0 5.7 %collective-permute-start.3 = (f32[6,28,1,128]{3,1,2,0:T(8,128)S(1)}, f32[6,28,1,128]{3,1,2,0:T(8,128)S(1)}, u32[]{:S(2)}, u32[]{:S(2)}) collective-permute-start(f32[6,28,1,128]{3,1,2,0:T(8,128)S(1)} %copy.38), channel_id=1, source_target_pairs={{1,0},{0,1},{3,2},{2,3},{5,4},{4,5},{7,6},{6,7},{9,8},{8,9},{11,10... | collective-permute-start | bytes 258056 | tf_op jit(solution)/shard_map/ppermute | solution.py:31
  24.5 7.3 %collective-permute-start.4 = (f32[6,28,1,128]{3,1,2,0:T(8,128)S(1)}, f32[6,28,1,128]{3,1,2,0:T(8,128)S(1)}, u32[]{:S(2)}, u32[]{:S(2)}) collective-permute-start(f32[6,28,1,128]{3,1,2,0:T(8,128)S(1)} %copy.40), channel_id=1, source_target_pairs={{0,1},{1,0},{2,3},{3,2},{4,5},{5,4},{6,7},{7,6},{8,9},{9,8},{10,11... | collective-permute-start | bytes 258056 | tf_op jit(solution)/shard_map/ppermute | solution.py:29
  33.0 0.7 %copy-start.5 = (f32[7]{0:T(128)S(1)}, f32[7]{0:T(128)}, u32[]{:S(2)}) copy-start(f32[7]{0:T(128)} %constant.52.clone) | copy-start | bytes 88
  34.5 5.7 %collective-permute-start.5 = (f32[6,26,1,128]{3,1,2,0:T(8,128)S(1)}, f32[6,26,1,128]{3,1,2,0:T(8,128)S(1)}, u32[]{:S(2)}, u32[]{:S(2)}) collective-permute-start(f32[6,26,1,128]{3,1,2,0:T(8,128)S(1)} %copy.42), channel_id=1, source_target_pairs={{1,0},{0,1},{3,2},{2,3},{5,4},{4,5},{7,6},{6,7},{9,8},{8,9},{11,10... | collective-permute-start | bytes 239624 | tf_op jit(solution)/shard_map/ppermute | solution.py:31
  34.6 6.9 %collective-permute-start.6 = (f32[6,26,1,128]{3,1,2,0:T(8,128)S(1)}, f32[6,26,1,128]{3,1,2,0:T(8,128)S(1)}, u32[]{:S(2)}, u32[]{:S(2)}) collective-permute-start(f32[6,26,1,128]{3,1,2,0:T(8,128)S(1)} %copy.44), channel_id=1, source_target_pairs={{0,1},{1,0},{2,3},{3,2},{4,5},{5,4},{6,7},{7,6},{8,9},{9,8},{10,11... | collective-permute-start | bytes 239624 | tf_op jit(solution)/shard_map/ppermute | solution.py:29
where the time goes:
time: 44.5 us; the launch traced here: 44.3 us
  waiting for transfers between devices  20.9 us (47%)
  other arithmetic  10.4 us (23%)
  starting transfers between devices  8.36 us (19%)
  local copies, waits for them, and re-layouts  3.54 us (8%)
  between operations  1.07 us (2%)
    ppermute x3, waiting for transfers between devices, padded_2(): lax.ppermute(head, axis, [((i + 1) % count, i) for i in range(count)])  8.93 us
    ppermute x1, waiting for transfers between devices, from_behind(): lax.ppermute(value, axis, [(source, source + steps) for source in range(i...  6.34 us
    ppermute x3, waiting for transfers between devices, padded_2(): lax.ppermute(tail, axis, [(i, (i + 1) % count) for i in range(count)])  5.61 us
    ppermute x3, starting transfers between devices, padded_2(): lax.ppermute(tail, axis, [(i, (i + 1) % count) for i in range(count)])  4.29 us
    ppermute x3, starting transfers between devices, padded_2(): lax.ppermute(head, axis, [((i + 1) % count, i) for i in range(count)])  2.15 us
    ppermute x1, starting transfers between devices, from_behind(): lax.ppermute(value, axis, [(source, source + steps) for source in range(i...  1.92 us
    reduce_sum x3, other arithmetic, advance(): jnp.mean(forcing, axis=0, keepdims=True)  1.87 us
    sub x3, other arithmetic, advance(): new_solutes = solutes + TIME_STEP * influx - rejected  1.73 us
  transfers between devices with their start and end apart: 7, of which 7 were waited for; matrix products, arithmetic and copies ran while one was open for 3% of the time, Pallas kernels for 0%

commit v1 on v0

v1 whole, which is shorter than its diff:
```python
import functools

import jax
import jax.numpy as jnp
from jax import lax
from jax.experimental import pallas as pl
from jax.experimental.pallas import tpu as pltpu
from jax.sharding import PartitionSpec as P

SHIFT = 16
STEPS = 3

PHASES = 4
SOLUTES = 2
FIELDS = PHASES + SOLUTES
RAW = 4

ANISOTROPY = 1.5
WELL_HEIGHT = 4.0
TIME_STEP = 0.06
LIQUID_DIFFUSION = 1.0
SOLID_DIFFUSION = 0.1
COOLING_WEIGHTS = (-1.0, 0.8, 0.7, 0.6)
FIRST_WEIGHTS = (0.5, -1.0, 0.4, 0.3)
SECOND_WEIGHTS = (0.4, 0.3, -1.0, 0.5)
INFLOW = (1.0, 0.0, 0.0, 0.0, 0.3, 0.2)
LIQUID_MOBILITY = 1.0

F32 = jnp.float32


class Plan:
    def __init__(self, planes, rows, slabs, blocks):
        self.planes, self.rows, self.slabs, self.blocks = planes, rows, slabs, blocks
        self.own = planes - SHIFT + STEPS
        self.next = SHIFT + STEPS
        self.depth = self.own + self.next
        self.pitch = (rows + 2 * STEPS) | 1
        self.window_rows = -(-self.depth * self.pitch // 8) * 8
        self.own_pieces, self.own_rows = self.pieces(0, self.own)
        self.next_pieces, self.next_rows = self.pieces(self.own, self.depth)

    def pieces(self, first, last):
        found, lengths = [], []
        for side in range(2):
            if self.blocks > 2 or not lengths:
                lengths.append(0)
            for j in range(first, last):
                for array in range(RAW):
                    inset = 1 if array == 3 else 0
                    count = min(STEPS - inset, j - inset, self.depth - 1 - inset - j)
                    if count > 0:
                        found.append((side, array, j, count, len(lengths) - 1, lengths[-1]))
                        lengths[-1] += count
        return found, [-(-length // 8) * 8 for length in lengths]


def pack_kernel(plan, phase, grain, solutes, orient, mobil, own, grow, *halos):
    rows = plan.rows
    table = jnp.zeros((rows, 128), F32)
    lanes = lax.broadcasted_iota(jnp.int32, (rows, 128), 1)
    for g in range(orient.shape[0]):
        table = jnp.where(lanes == g, mobil[orient[g]], table)
    own_halos = halos[: len(plan.own_rows)]
    next_halos = halos[len(plan.own_rows) :]
    first = SHIFT - STEPS
    where = {}
    for pieces, buffers, shift in ((plan.own_pieces, own_halos, first), (plan.next_pieces, next_halos, -plan.own)):
        for side, array, j, count, buffer, offset in pieces:
            where.setdefault((array, j + shift), []).append((side, count, buffers[buffer], offset))
    for z in range(plan.planes):
        label = phase[z].astype(F32)
        mobility = jnp.take_along_axis(table, grain[z], axis=1)
        for array, tile in enumerate((label, solutes[0, z], solutes[1, z], mobility)):
            if z >= first:
                own[array, z - first] = tile
            if z < plan.next:
                grow[array, z] = tile
            for side, count, buffer, offset in where.get((array, z), ()):
                piece = tile[:count] if side == 0 else tile[rows - count :]
                buffer[offset : offset + count, :] = piece


def step_tile(load, undercool, mobility, partition):
    centre = [load(f, 0, 0) for f in range(FIELDS)]
    below = [load(f, -1, 0) for f in range(FIELDS)]
    above = [load(f, 1, 0) for f in range(FIELDS)]
    prev = [load(f, 0, -1) for f in range(FIELDS)]
    after = [load(f, 0, 1) for f in range(FIELDS)]
    left = [pltpu.roll(c, 1, 1) for c in centre]
    right = [pltpu.roll(c, c.shape[1] - 1, 1) for c in centre]
    c0, c1 = centre[4], centre[5]
    forcing = []
    for a in range(PHASES):
        p = centre[a]
        laplace = ANISOTROPY * (above[a] + below[a]) + ((prev[a] + after[a]) + (left[a] + right[a]))
        laplace = laplace - (2.0 * ANISOTROPY + 4.0) * p
        driving = (COOLING_WEIGHTS[a] * undercool - 0.5) + FIRST_WEIGHTS[a] * c0 + SECOND_WEIGHTS[a] * c1
        well = WELL_HEIGHT * p
        forcing.append(laplace + (well - well * p) * (p + driving))
    mean = 0.25 * ((forcing[0] + forcing[1]) + (forcing[2] + forcing[3]))
    rate = TIME_STEP * mobility
    trials = [jnp.clip(centre[a] + rate * (forcing[a] - mean), 0.0, 1.0) for a in range(PHASES)]
    scale = 1.0 / ((trials[0] + trials[1]) + (trials[2] + trials[3]))
    phases = [t * scale for t in trials]
    slope = 0.5 * TIME_STEP * (LIQUID_DIFFUSION - SOLID_DIFFUSION)
    base = 0.5 * TIME_STEP * 2.0 * SOLID_DIFFUSION
    own = slope * centre[0] + base
    inflow = [None, None]
    for side in (above, below, prev, after, left, right):
        both = slope * side[0] + own
        for k in range(SOLUTES):
            flux = both * (side[4 + k] - centre[4 + k])
            inflow[k] = flux if inflow[k] is None else inflow[k] + flux
    changes = [phases[a] - centre[a] for a in range(PHASES)]
    solutes = []
    for k in range(SOLUTES):
        rejected = (partition[0, k] * changes[0] + partition[1, k] * changes[1]) + (
            partition[2, k] * changes[2] + partition[3, k] * changes[3]
        )
        solutes.append(centre[4 + k] + (inflow[k] - rejected))
    return phases + solutes


def main_kernel(plan, own, grow, partition, *refs):
    n_own, n_next = len(plan.own_rows), len(plan.next_rows)
    own_halos, next_halos = refs[:n_own], refs[n_own : n_own + n_next]
    phase_out, solute_out, field_a, field_b, mob, result, sems = refs[n_own + n_next :]
    rows, pitch, depth = plan.rows, plan.pitch, plan.depth
    slab = lax.axis_index("grow")
    first_slab, last_slab = slab == 0, slab == plan.slabs - 1
    edge = plan.own - 1
    total = plan.planes * plan.slabs

    def put(array, j, row, count, tile):
        spot = pl.ds(j * pitch + row, count)
        if array == 0:
            for a in range(PHASES):
                field_a[a, spot, :] = jnp.where(tile == a, 1.0, 0.0)
        elif array == 3:
            mob[spot, :] = tile
        else:
            field_a[PHASES - 1 + array, spot, :] = tile

    for j in range(depth):
        for array in range(RAW):
            tile = own[array, j] if j < plan.own else grow[array, j - plan.own]
            put(array, j, STEPS, rows, tile)
    for pieces, buffers in ((plan.own_pieces, own_halos), (plan.next_pieces, next_halos)):
        for side, array, j, count, buffer, offset in pieces:
            row = STEPS + rows if side == 0 else STEPS - count
            put(array, j, row, count, buffers[buffer][offset : offset + count, :])

    def repeat_edge(fields, source, target):
        for f in range(FIELDS):
            for row in (0, pitch - 8):
                fields[f, pl.ds(target * pitch + row, 8), :] = fields[f, pl.ds(source * pitch + row, 8), :]

    def sweep(source, target, begin, end, starts, base, mob_shift):
        def body(j, carry):
            height = (base + j).astype(F32)
            undercool = 2.0 * (0.5 - (height + 0.5) * (1.0 / total))
            for start in starts:
                at = j * pitch + start

                def load(f, dz, dr):
                    return source[f, pl.ds(at + dz * pitch + dr, 8), :]

                new = step_tile(load, undercool, mob[pl.ds(at, 8), :], partition)
                if target is None:
                    for f in range(FIELDS):
                        result[f, j - STEPS] = new[f]
                else:
                    for f in range(FIELDS):
                        target[f, pl.ds(at, 8), :] = new[f]
            return carry

        lax.fori_loop(begin, end, body, 0)

    origin = slab * plan.planes + SHIFT - STEPS

    @pl.when(last_slab)
    def _():
        repeat_edge(field_a, edge, edge + 1)

    sweep(field_a, field_b, 1, depth - 1, (1, rows + 2 * STEPS - 9), origin, 0)

    @pl.when(last_slab)
    def _():
        repeat_edge(field_b, edge, edge + 1)

    sweep(field_b, field_a, 2, depth - 2, (2, rows + 2 * STEPS - 10), origin, 0)

    @pl.when(last_slab)
    def _():
        for j in range(edge + 1, depth - 2):
            for row in (0, pitch - 8):
                spot = pl.ds(j * pitch + row, 8)
                for f in range(FIELDS):
                    field_a[f, spot, :] = jnp.full((8, 128), INFLOW[f], F32)
                mob[spot, :] = jnp.full((8, 128), LIQUID_MOBILITY, F32)

    @pl.when(first_slab)
    def _():
        repeat_edge(field_a, STEPS, STEPS - 1)

    sweep(field_a, None, STEPS, depth - STEPS, (STEPS,), slab * plan.planes - STEPS, 0)
    copies = (
        pltpu.make_async_copy(result.at[pl.ds(0, PHASES)], phase_out, sems.at[0]),
        pltpu.make_async_copy(result.at[pl.ds(PHASES, SOLUTES)], solute_out, sems.at[1]),
    )
    for copy in copies:
        copy.start()
    for copy in copies:
        copy.wait()


def shards(phase_label, grain_label, grain_orient, orient_mobility, solute_init, partition):
    slabs, blocks = lax.axis_size("grow"), lax.axis_size("trans")
    planes, rows, columns = phase_label.shape
    plan = Plan(planes, rows, slabs, blocks)
    vmem, smem, hbm = (pl.BlockSpec(memory_space=m) for m in (pltpu.VMEM, pltpu.SMEM, pl.ANY))
    halo_shapes = [
        jax.ShapeDtypeStruct((length, columns), F32) for length in plan.own_rows + plan.next_rows
    ]
    own, grow, *halos = pl.pallas_call(
        functools.partial(pack_kernel, plan),
        out_shape=[
            jax.ShapeDtypeStruct((RAW, plan.own, rows, columns), F32),
            jax.ShapeDtypeStruct((RAW, plan.next, rows, columns), F32),
            *halo_shapes,
        ],
        in_specs=[vmem, vmem, vmem, smem, smem],
        out_specs=[vmem] * (2 + len(halo_shapes)),
        name="pack",
    )(phase_label, grain_label, solute_init, grain_orient, orient_mobility)

    ups = [(b + 1) % blocks for b in range(blocks)]
    downs = [(b - 1) % blocks for b in range(blocks)]

    def fetch(value, side, hop):
        others = ups if side == 0 else downs
        pairs = [
            ((s + hop) * blocks + others[b], s * blocks + b) for s in range(slabs - hop) for b in range(blocks)
        ]
        return lax.ppermute(value, ("grow", "trans"), pairs)

    n_own = len(plan.own_rows)
    own_halos = [fetch(value, side, 0) for side, value in enumerate(halos[:n_own])]
    next_halos = [fetch(value, side, 1) for side, value in enumerate(halos[n_own:])]
    received = lax.ppermute(grow, "grow", [(s + 1, s) for s in range(slabs - 1)])

    fields = pltpu.VMEM((FIELDS, plan.window_rows, columns), F32)
    return pl.pallas_call(
        functools.partial(main_kernel, plan),
        out_shape=[
            jax.ShapeDtypeStruct((PHASES, planes, rows, columns), F32),
            jax.ShapeDtypeStruct((SOLUTES, planes, rows, columns), F32),
        ],
        in_specs=[vmem, vmem, smem] + [vmem] * len(halos),
        out_specs=[hbm, hbm],
        scratch_shapes=[
            fields,
            fields,
            pltpu.VMEM((plan.window_rows, columns), F32),
            pltpu.VMEM((FIELDS, planes, rows, columns), F32),
            pltpu.SemaphoreType.DMA((2,)),
        ],
        name="steps",
    )(own, received, partition, *own_halos, *next_halos)


def solution(mesh):
    placed = (
        P("grow", "trans", None),
        P("grow", "trans", None),
        P(),
        P(),
        P(None, "grow", "trans", None),
        P(),
    )
    return jax.shard_map(
        shards,
        mesh=mesh,
        in_specs=placed,
        out_specs=(P(None, "grow", "trans", None), P(None, "grow", "trans", None)),
        check_vma=False,
    )
```

time: 44.5 us -> 28.8 us (0.65)
  the two profiles are of different devices: /device:TPU:4 before, /device:TPU:9 now
where the time goes in v1:
time: 28.8 us; the launch traced here: 28.6 us
  Pallas kernels  12.9 us (45%)
  waiting for transfers between devices  6.82 us (24%)
  starting transfers between devices  6.74 us (23%)
  local copies, waits for them, and re-layouts  1.49 us (5%)
  between operations  0.67 us (2%)
    pallas_call x1, Pallas kernels, shards(): pl.pallas_call(functools.partial(main_kernel, plan), out_shape=[jax.Shape...  10.9 us
    ppermute x2, waiting for transfers between devices, fetch(): return lax.ppermute(value, ('grow', 'trans'), pairs)  6.81 us
    ppermute x2, starting transfers between devices, fetch(): return lax.ppermute(value, ('grow', 'trans'), pairs)  4.17 us
    ppermute x1, starting transfers between devices, shards(): lax.ppermute(grow, 'grow', [(s + 1, s) for s in range(slabs - 1)])  2.57 us
    pallas_call x1, Pallas kernels, shards(): pl.pallas_call(functools.partial(pack_kernel, plan), out_shape=[jax.Shape...  2.04 us
    unnamed x9, local copies, waits for them, and re-layouts  1.49 us
  transfers between devices with their start and end apart: 3, of which 1 were waited for; matrix products, arithmetic and copies ran while one was open for 2% of the time, Pallas kernels for 0%

profile of v1, /device:TPU:9, one launch (start us, length us, event | category | flops | bytes accessed | tf_op | source)
XLA Modules:
  0.0 28.6 jit_solution(15672662124199533278)
XLA Ops:
  0.6 2.0 %pack.1 = (f32[4,11,8,128]{3,2,1,0:T(8,128)}, f32[4,19,8,128]{3,2,1,0:T(8,128)}, f32[200,128]{1,0:T(8,128)}, f32[376,128]{1,0:T(8,128)}) custom-call(s32[24,8,128]{2,1,0:T(8,128)} %phase.1, s32[24,8,128]{2,1,0:T(8,128)} %grain.1, f32[2,24,8,128]{3,2,1,0:T(8,128)} %solutes.1, s32[32]{0:T(128)} %orient.1, f32[8]{0:T(128)} %mobil.1), custom_call_target="tpu_custom_call" | custom-call | tf_op jit(solution)/shard_map/pack/pallas_call | solution.py:226
  2.7 2.6 %collective-permute-start = (f32[4,19,8,128]{3,2,1,0:T(8,128)}, f32[4,19,8,128]{3,2,1,0:T(8,128)S(1)}, u32[]{:S(2)}, u32[]{:S(2)}) collective-permute-start(f32[4,19,8,128]{3,2,1,0:T(8,128)} %get-tuple-element.7), channel_id=1, source_target_pairs={{2,0},{4,2},{6,4},{8,6},{10,8},{12,10},{14,12},{16,14},{18,16},{20... | collective-permute-start | bytes 933896 | tf_op jit(solution)/shard_map/ppermute | solution.py:251
  5.2 0.0 copy-start.3
  5.3 3.8 %collective-permute-start.2 = (f32[376,128]{1,0:T(8,128)}, f32[376,128]{1,0:T(8,128)S(1)}, u32[]{:S(2)}, u32[]{:S(2)}) collective-permute-start(f32[376,128]{1,0:T(8,128)} %get-tuple-element.9), channel_id=1, source_target_pairs={{3,0},{2,1},{5,2},{4,3},{7,4},{6,5},{9,6},{8,7},{11,8},{10,9},{13,... | collective-permute-start | bytes 577544 | tf_op jit(solution)/shard_map/ppermute | solution.py:246
  9.1 0.3 %collective-permute-start.1 = (f32[200,128]{1,0:T(8,128)}, f32[200,128]{1,0:T(8,128)S(1)}, u32[]{:S(2)}, u32[]{:S(2)}) collective-permute-start(f32[200,128]{1,0:T(8,128)} %get-tuple-element.8), channel_id=1, source_target_pairs={{1,0},{0,1},{3,2},{2,3},{5,4},{4,5},{7,6},{6,7},{9,8},{8,9},{11,10... | collective-permute-start | bytes 307208 | tf_op jit(solution)/shard_map/ppermute | solution.py:246
  9.4 0.0 copy-done.3
  9.4 0.7 %copy.8.partition = f32[4,2]{1,0:T(4,128)} copy(f32[4,2]{0,1:T(2,128)S(1)} %copy-done.3) | data formatting | bytes 64 | tf_op args[5]
  10.1 6.8 %collective-permute-done.1.refs_0_ = f32[200,128]{1,0:T(8,128)S(1)} collective-permute-done((f32[200,128]{1,0:T(8,128)}, f32[200,128]{1,0:T(8,128)S(1)}, u32[]{:S(2)}, u32[]{:S(2)}) %collective-permute-start.1) | collective-permute-done | bytes 102432 | tf_op jit(solution)/shard_map/ppermute | solution.py:246
  16.9 0.0 copy-start.2
  16.9 0.0 collective-permute-done.2.refs_1_
  16.9 0.0 copy-start.1
  16.9 0.0 collective-permute-done.grow
  16.9 0.0 copy-start
  16.9 0.6 %copy-done.2 = f32[200,128]{1,0:T(8,128)} copy-done((f32[200,128]{1,0:T(8,128)}, f32[200,128]{1,0:T(8,128)S(1)}, u32[]{:S(2)}) %copy-start.2) | copy-done | bytes 102424
  17.6 0.1 copy-done.1
  17.7 0.1 copy-done
  17.8 10.9 %steps.1 = (f32[4,24,8,128]{3,2,1,0:T(8,128)}, f32[2,24,8,128]{3,2,1,0:T(8,128)}) custom-call(f32[4,11,8,128]{3,2,1,0:T(8,128)} %get-tuple-element.6.own, f32[4,19,8,128]{3,2,1,0:T(8,128)} %copy-done, f32[4,2]{1,0:T(4,128)} %copy.8.partition, f32[200,128]{1,0:T(8,128)} %copy-done.2, f32[376,128]{1,0:T(8,128)} %copy-done.1), custom_call_target="tpu_custom_call" | custom-call | tf_op jit(solution)/shard_map/steps/pallas_call | solution.py:254
Async XLA Ops:
  2.7 14.3 %collective-permute-start = (f32[4,19,8,128]{3,2,1,0:T(8,128)}, f32[4,19,8,128]{3,2,1,0:T(8,128)S(1)}, u32[]{:S(2)}, u32[]{:S(2)}) collective-permute-start(f32[4,19,8,128]{3,2,1,0:T(8,128)} %get-tuple-element.7), channel_id=1, source_target_pairs={{2,0},{4,2},{6,4},{8,6},{10,8},{12,10},{14,12},{16,14},{18,16},{20... | collective-permute-start | bytes 933896 | tf_op jit(solution)/shard_map/ppermute | solution.py:251
  5.2 4.2 %copy-start.3 = (f32[4,2]{0,1:T(2,128)S(1)}, f32[4,2]{0,1:T(2,128)}, u32[]{:S(2)}) copy-start(f32[4,2]{0,1:T(2,128)} %param.11) | copy-start | bytes 100
  5.3 11.7 %collective-permute-start.2 = (f32[376,128]{1,0:T(8,128)}, f32[376,128]{1,0:T(8,128)S(1)}, u32[]{:S(2)}, u32[]{:S(2)}) collective-permute-start(f32[376,128]{1,0:T(8,128)} %get-tuple-element.9), channel_id=1, source_target_pairs={{3,0},{2,1},{5,2},{4,3},{7,4},{6,5},{9,6},{8,7},{11,8},{10,9},{13,... | collective-permute-start | bytes 577544 | tf_op jit(solution)/shard_map/ppermute | solution.py:246
  9.1 7.8 %collective-permute-start.1 = (f32[200,128]{1,0:T(8,128)}, f32[200,128]{1,0:T(8,128)S(1)}, u32[]{:S(2)}, u32[]{:S(2)}) collective-permute-start(f32[200,128]{1,0:T(8,128)} %get-tuple-element.8), channel_id=1, source_target_pairs={{1,0},{0,1},{3,2},{2,3},{5,4},{4,5},{7,6},{6,7},{9,8},{8,9},{11,10... | collective-permute-start | bytes 307208 | tf_op jit(solution)/shard_map/ppermute | solution.py:246
  16.9 0.6 %copy-start.2 = (f32[200,128]{1,0:T(8,128)}, f32[200,128]{1,0:T(8,128)S(1)}, u32[]{:S(2)}) copy-start(f32[200,128]{1,0:T(8,128)S(1)} %collective-permute-done.1.refs_0_) | copy-start | bytes 307204
  16.9 0.7 %copy-start.1 = (f32[376,128]{1,0:T(8,128)}, f32[376,128]{1,0:T(8,128)S(1)}, u32[]{:S(2)}) copy-start(f32[376,128]{1,0:T(8,128)S(1)} %collective-permute-done.2.refs_1_) | copy-start | bytes 577540
  16.9 0.8 %copy-start = (f32[4,19,8,128]{3,2,1,0:T(8,128)}, f32[4,19,8,128]{3,2,1,0:T(8,128)S(1)}, u32[]{:S(2)}) copy-start(f32[4,19,8,128]{3,2,1,0:T(8,128)S(1)} %collective-permute-done.grow) | copy-start | bytes 933892

commit v2 on v1

--- a/solution.py
+++ b/solution.py
@@ -6,6 +6,7 @@
 from jax.experimental import pallas as pl
 from jax.experimental.pallas import tpu as pltpu
 from jax.sharding import PartitionSpec as P
+
 
 SHIFT = 16
 STEPS = 3
@@ -115,8 +116,8 @@
     changes = [phases[a] - centre[a] for a in range(PHASES)]
     solutes = []
     for k in range(SOLUTES):
-        rejected = (partition[0, k] * changes[0] + partition[1, k] * changes[1]) + (
-            partition[2, k] * changes[2] + partition[3, k] * changes[3]
+        rejected = (partition[k, 0] * changes[0] + partition[k, 1] * changes[1]) + (
+            partition[k, 2] * changes[2] + partition[k, 3] * changes[3]
         )
         solutes.append(centre[4 + k] + (inflow[k] - rejected))
     return phases + solutes
@@ -156,7 +157,7 @@
             for row in (0, pitch - 8):
                 fields[f, pl.ds(target * pitch + row, 8), :] = fields[f, pl.ds(source * pitch + row, 8), :]
 
-    def sweep(source, target, begin, end, starts, base, mob_shift):
+    def sweep(source, target, begin, end, starts, base):
         def body(j, carry):
             height = (base + j).astype(F32)
             undercool = 2.0 * (0.5 - (height + 0.5) * (1.0 / total))
@@ -175,7 +176,8 @@
                         target[f, pl.ds(at, 8), :] = new[f]
             return carry
 
-        lax.fori_loop(begin, end, body, 0)
+        for j in range(begin, end):
+            body(j, 0)
 
     origin = slab * plan.planes + SHIFT - STEPS
 
@@ -183,13 +185,13 @@
     def _():
         repeat_edge(field_a, edge, edge + 1)
 
-    sweep(field_a, field_b, 1, depth - 1, (1, rows + 2 * STEPS - 9), origin, 0)
+    sweep(field_a, field_b, 1, depth - 1, (1, rows + 2 * STEPS - 9), origin)
 
     @pl.when(last_slab)
     def _():
         repeat_edge(field_b, edge, edge + 1)
 
-    sweep(field_b, field_a, 2, depth - 2, (2, rows + 2 * STEPS - 10), origin, 0)
+    sweep(field_b, field_a, 2, depth - 2, (2, rows + 2 * STEPS - 10), origin)
 
     @pl.when(last_slab)
     def _():
@@ -204,7 +206,7 @@
     def _():
         repeat_edge(field_a, STEPS, STEPS - 1)
 
-    sweep(field_a, None, STEPS, depth - STEPS, (STEPS,), slab * plan.planes - STEPS, 0)
+    sweep(field_a, None, STEPS, depth - STEPS, (STEPS,), slab * plan.planes - STEPS)
     copies = (
         pltpu.make_async_copy(result.at[pl.ds(0, PHASES)], phase_out, sems.at[0]),
         pltpu.make_async_copy(result.at[pl.ds(PHASES, SOLUTES)], solute_out, sems.at[1]),
@@ -215,19 +217,23 @@
         copy.wait()
 
 
+def on_chip(value):
+    return pltpu.with_memory_space_constraint(value, pltpu.VMEM)
+
+
 def shards(phase_label, grain_label, grain_orient, orient_mobility, solute_init, partition):
     slabs, blocks = lax.axis_size("grow"), lax.axis_size("trans")
     planes, rows, columns = phase_label.shape
     plan = Plan(planes, rows, slabs, blocks)
     vmem, smem, hbm = (pl.BlockSpec(memory_space=m) for m in (pltpu.VMEM, pltpu.SMEM, pl.ANY))
     halo_shapes = [
-        jax.ShapeDtypeStruct((length, columns), F32) for length in plan.own_rows + plan.next_rows
+        pltpu.VMEM((length, columns), F32) for length in plan.own_rows + plan.next_rows
     ]
     own, grow, *halos = pl.pallas_call(
         functools.partial(pack_kernel, plan),
         out_shape=[
-            jax.ShapeDtypeStruct((RAW, plan.own, rows, columns), F32),
-            jax.ShapeDtypeStruct((RAW, plan.next, rows, columns), F32),
+            pltpu.VMEM((RAW, plan.own, rows, columns), F32),
+            pltpu.VMEM((RAW, plan.next, rows, columns), F32),
             *halo_shapes,
         ],
         in_specs=[vmem, vmem, vmem, smem, smem],
@@ -267,7 +273,7 @@
             pltpu.SemaphoreType.DMA((2,)),
         ],
         name="steps",
-    )(own, received, partition, *own_halos, *next_halos)
+    )(*(on_chip(x) for x in (own, received)), partition.T, *(on_chip(x) for x in own_halos + next_halos))
 
 
 def solution(mesh):

time: 28.8 us -> 21.1 us (0.73)
  Pallas kernels: 12.9 us -> 6.21 us
  local copies, waits for them, and re-layouts: 1.49 us -> 0 us
  waiting for transfers between devices: 6.82 us -> 7.28 us
    pallas_call x1, Pallas kernels: 10.9 us -> 5.02 us  [shards(): pl.pallas_call(functools.partial(main_kernel, plan), out_shape=[jax.Shape...]
    unnamed x9 -> x0, local copies, waits for them, and re-layouts: 1.49 us -> none
    pallas_call x1, Pallas kernels: 2.04 us -> 1.19 us  [shards(): pl.pallas_call(functools.partial(pack_kernel, plan), out_shape=[pltpu.VME...]
    ppermute x2, waiting for transfers between devices: 6.81 us -> 7.27 us  [fetch(): return lax.ppermute(value, ('grow', 'trans'), pairs)]
  transfers between devices with their start and end apart: 3 -> 3, of which waited for: 1 -> 1; matrix products, arithmetic and copies ran while one was open for 2% -> 0% of each run, Pallas kernels for 0% -> 0%
where the time goes in v2:
time: 21.1 us; the launch traced here: 20.9 us
  waiting for transfers between devices  7.28 us (35%)
  starting transfers between devices  6.75 us (32%)
  Pallas kernels  6.21 us (29%)
  between operations  0.65 us (3%)
    ppermute x2, waiting for transfers between devices, fetch(): return lax.ppermute(value, ('grow', 'trans'), pairs)  7.27 us
    pallas_call x1, Pallas kernels, shards(): pl.pallas_call(functools.partial(main_kernel, plan), out_shape=[jax.Shape...  5.02 us
    ppermute x2, starting transfers between devices, fetch(): return lax.ppermute(value, ('grow', 'trans'), pairs)  4.17 us
    ppermute x1, starting transfers between devices, shards(): lax.ppermute(grow, 'grow', [(s + 1, s) for s in range(slabs - 1)])  2.58 us
    pallas_call x1, Pallas kernels, shards(): pl.pallas_call(functools.partial(pack_kernel, plan), out_shape=[pltpu.VME...  1.19 us
  transfers between devices with their start and end apart: 3, of which 1 were waited for; matrix products, arithmetic and copies ran while one was open for 0% of the time, Pallas kernels for 0%

profile of v2, /device:TPU:9, one launch (start us, length us, event | category | flops | bytes accessed | tf_op | source)
XLA Modules:
  0.0 20.9 jit_solution(1433650799658297014)
XLA Ops:
  0.6 1.2 %pack.1 = (f32[4,11,8,128]{3,2,1,0:T(8,128)S(1)}, f32[4,19,8,128]{3,2,1,0:T(8,128)S(1)}, f32[200,128]{1,0:T(8,128)S(1)}, f32[376,128]{1,0:T(8,128)S(1)}) custom-call(s32[24,8,128]{2,1,0:T(8,128)} %phase.1, s32[24,8,128]{2,1,0:T(8,128)} %grain.1, f32[2,24,8,128]{3,2,1,0:T(8,128)} %solutes.1, s32[32]{0:T(128)} %orient.1, f32[8]{0:T(128)} %mobil.1), custom_call_target="tpu_custom_call" | custom-call | tf_op jit(solution)/shard_map/pack/pallas_call | solution.py:232
  1.8 2.6 %collective-permute-start = (f32[4,19,8,128]{3,2,1,0:T(8,128)S(1)}, f32[4,19,8,128]{3,2,1,0:T(8,128)S(1)}, u32[]{:S(2)}, u32[]{:S(2)}) collective-permute-start(f32[4,19,8,128]{3,2,1,0:T(8,128)S(1)} %get-tuple-element.7), channel_id=1, source_target_pairs={{2,0},{4,2},{6,4},{8,6},{10,8},{12,10},{14,12},{16,14},{18,16},{20... | collective-permute-start | bytes 933896 | tf_op jit(solution)/shard_map/ppermute | solution.py:257
  4.4 3.8 %collective-permute-start.2 = (f32[376,128]{1,0:T(8,128)S(1)}, f32[376,128]{1,0:T(8,128)S(1)}, u32[]{:S(2)}, u32[]{:S(2)}) collective-permute-start(f32[376,128]{1,0:T(8,128)S(1)} %get-tuple-element.9), channel_id=1, source_target_pairs={{3,0},{2,1},{5,2},{4,3},{7,4},{6,5},{9,6},{8,7},{11,8},{10,9},{13,... | collective-permute-start | bytes 577544 | tf_op jit(solution)/shard_map/ppermute | solution.py:252
  8.3 0.3 %collective-permute-start.1 = (f32[200,128]{1,0:T(8,128)S(1)}, f32[200,128]{1,0:T(8,128)S(1)}, u32[]{:S(2)}, u32[]{:S(2)}) collective-permute-start(f32[200,128]{1,0:T(8,128)S(1)} %get-tuple-element.8), channel_id=1, source_target_pairs={{1,0},{0,1},{3,2},{2,3},{5,4},{4,5},{7,6},{6,7},{9,8},{8,9},{11,10... | collective-permute-start | bytes 307208 | tf_op jit(solution)/shard_map/ppermute | solution.py:252
  8.6 7.3 %collective-permute-done.1.refs_0_ = f32[200,128]{1,0:T(8,128)S(1)} collective-permute-done((f32[200,128]{1,0:T(8,128)S(1)}, f32[200,128]{1,0:T(8,128)S(1)}, u32[]{:S(2)}, u32[]{:S(2)}) %collective-permute-start.1) | collective-permute-done | bytes 102432 | tf_op jit(solution)/shard_map/ppermute | solution.py:252
  15.9 0.0 collective-permute-done.2.refs_1_
  15.9 0.0 collective-permute-done.grow
  15.9 5.0 %steps.1 = (f32[4,24,8,128]{3,2,1,0:T(8,128)}, f32[2,24,8,128]{3,2,1,0:T(8,128)}) custom-call(f32[4,11,8,128]{3,2,1,0:T(8,128)S(1)} %get-tuple-element.6.own, f32[4,19,8,128]{3,2,1,0:T(8,128)S(1)} %collective-permute-done.grow, f32[2,4]{1,0:T(2,128)} %bitcast.1, f32[200,128]{1,0:T(8,128)S(1)} %collective-permute-done.1.refs_0_, ...), custom_call_target="tpu_custom_call" | custom-call | tf_op jit(solution)/shard_map/steps/pallas_call | solution.py:260
Async XLA Ops:
  1.8 14.0 %collective-permute-start = (f32[4,19,8,128]{3,2,1,0:T(8,128)S(1)}, f32[4,19,8,128]{3,2,1,0:T(8,128)S(1)}, u32[]{:S(2)}, u32[]{:S(2)}) collective-permute-start(f32[4,19,8,128]{3,2,1,0:T(8,128)S(1)} %get-tuple-element.7), channel_id=1, source_target_pairs={{2,0},{4,2},{6,4},{8,6},{10,8},{12,10},{14,12},{16,14},{18,16},{20... | collective-permute-start | bytes 933896 | tf_op jit(solution)/shard_map/ppermute | solution.py:257
  4.4 11.5 %collective-permute-start.2 = (f32[376,128]{1,0:T(8,128)S(1)}, f32[376,128]{1,0:T(8,128)S(1)}, u32[]{:S(2)}, u32[]{:S(2)}) collective-permute-start(f32[376,128]{1,0:T(8,128)S(1)} %get-tuple-element.9), channel_id=1, source_target_pairs={{3,0},{2,1},{5,2},{4,3},{7,4},{6,5},{9,6},{8,7},{11,8},{10,9},{13,... | collective-permute-start | bytes 577544 | tf_op jit(solution)/shard_map/ppermute | solution.py:252
  8.3 7.6 %collective-permute-start.1 = (f32[200,128]{1,0:T(8,128)S(1)}, f32[200,128]{1,0:T(8,128)S(1)}, u32[]{:S(2)}, u32[]{:S(2)}) collective-permute-start(f32[200,128]{1,0:T(8,128)S(1)} %get-tuple-element.8), channel_id=1, source_target_pairs={{1,0},{0,1},{3,2},{2,3},{5,4},{4,5},{7,6},{6,7},{9,8},{8,9},{11,10... | collective-permute-start | bytes 307208 | tf_op jit(solution)/shard_map/ppermute | solution.py:252

commit v3 on v2

v3 whole, which is shorter than its diff:
```python
import functools

import jax
import jax.numpy as jnp
from jax import lax
from jax.experimental import pallas as pl
from jax.experimental.pallas import tpu as pltpu
from jax.sharding import PartitionSpec as P


SHIFT = 16
STEPS = 3

PHASES = 4
SOLUTES = 2
FIELDS = PHASES + SOLUTES
RAW = 4
TILE = 8

ANISOTROPY = 1.5
WELL_HEIGHT = 4.0
TIME_STEP = 0.06
LIQUID_DIFFUSION = 1.0
SOLID_DIFFUSION = 0.1
COOLING_WEIGHTS = (-1.0, 0.8, 0.7, 0.6)
FIRST_WEIGHTS = (0.5, -1.0, 0.4, 0.3)
SECOND_WEIGHTS = (0.4, 0.3, -1.0, 0.5)
INFLOW = (1.0, 0.0, 0.0, 0.0, 0.3, 0.2)
LIQUID_MOBILITY = 1.0

F32 = jnp.float32
PARAMS = pltpu.CompilerParams(vmem_limit_bytes=16 * 1024 * 1024)


def aligned(length):
    return -(-length // TILE) * TILE


class Plan:
    def __init__(self, planes, rows, slabs, blocks):
        self.planes, self.rows, self.slabs, self.blocks = planes, rows, slabs, blocks
        self.own = planes - SHIFT + STEPS
        self.next = SHIFT + STEPS
        self.depth = self.own + self.next
        self.wide = rows + 2 * STEPS
        self.pitch = aligned(self.depth + 2) + TILE
        self.total = planes * slabs
        self.own_runs, self.own_rows = self.runs(0, self.own)
        self.next_runs, self.next_rows = self.runs(self.own, self.depth)

    def runs(self, first, last):
        found, lengths = [], []
        for side in range(2):
            if self.blocks > 2 or not lengths:
                lengths.append(0)
            for array in range(RAW):
                inset = 1 if array == 3 else 0
                for distance in range(1, STEPS + 1 - inset):
                    low = max(first, distance + inset)
                    count = min(last, self.depth - distance - inset) - low
                    if count > 0:
                        found.append((side, array, distance, low, count, len(lengths) - 1, lengths[-1]))
                        lengths[-1] += count
        return found, [aligned(length) for length in lengths]

    def away(self, w):
        return max(0, STEPS - w, w - (STEPS + self.rows - 1))

    def starts(self, step, w):
        edge = step + self.away(w)
        low, high = edge, self.depth - edge
        return list(range(low, high - TILE, TILE)) + [high - TILE]


def pack_kernel(plan, *refs):
    inputs, (own, grow, rates, *halos), scratch = refs[:6], refs[6:-7], refs[-7:]
    *buffers, sems = scratch
    copies = [pltpu.make_async_copy(a, b, sems.at[i]) for i, (a, b) in enumerate(zip(inputs, buffers))]
    for copy in copies:
        copy.start()
    phase, grain, solutes, orient, mobil, partition = buffers
    for copy in copies[::-1]:
        copy.wait()
    rows = plan.rows
    for k in range(SOLUTES):
        for a in range(PHASES):
            rates[pl.ds((k * PHASES + a) * TILE, TILE), :] = jnp.full((TILE, 128), partition[k, a])
    table = jnp.zeros((rows, 128), F32)
    lanes = lax.broadcasted_iota(jnp.int32, (rows, 128), 1)
    for g in range(orient.shape[0]):
        table = jnp.where(lanes == g, mobil[orient[g]], table)
    first = SHIFT - STEPS
    for z in range(plan.planes):
        label = phase[z].astype(F32)
        mobility = jnp.take_along_axis(table, grain[z], axis=1)
        for array, tile in enumerate((label, solutes[0, z], solutes[1, z], mobility)):
            if z >= first:
                own[pl.ds((array * plan.own + z - first) * rows, rows), :] = tile
            if z < plan.next:
                grow[pl.ds((array * plan.next + z) * rows, rows), :] = tile
    n_own = len(plan.own_rows)
    for source, begin, length, runs, buffers in (
        (grow, plan.own, plan.next, plan.next_runs, halos[n_own:]),
        (own, 0, plan.own, plan.own_runs, halos[:n_own]),
    ):
        for side, array, distance, j, count, buffer, offset in runs:
            row = distance - 1 if side == 0 else rows - distance
            for k in range(0, count, TILE):
                n = min(TILE, count - k)
                at = (array * length + j - begin + k) * rows + row
                buffers[buffer][pl.ds(offset + k, n), :] = source[pl.ds(at, n, stride=rows), :]


def step_tile(load, cooling, mobility, partition):
    centre = [load(f, 0, 0) for f in range(FIELDS)]
    below = [load(f, -1, 0) for f in range(FIELDS)]
    above = [load(f, 1, 0) for f in range(FIELDS)]
    prev = [load(f, 0, -1) for f in range(FIELDS)]
    after = [load(f, 0, 1) for f in range(FIELDS)]
    left = [pltpu.roll(c, 1, 1) for c in centre]
    right = [pltpu.roll(c, c.shape[1] - 1, 1) for c in centre]
    c0, c1 = centre[4], centre[5]
    forcing = []
    for a in range(PHASES):
        p = centre[a]
        laplace = ANISOTROPY * (above[a] + below[a]) + ((prev[a] + after[a]) + (left[a] + right[a]))
        laplace = laplace - (2.0 * ANISOTROPY + 4.0) * p
        driving = cooling(a) + FIRST_WEIGHTS[a] * c0 + SECOND_WEIGHTS[a] * c1
        well = WELL_HEIGHT * p
        forcing.append(laplace + (well - well * p) * (p + driving))
    mean = 0.25 * ((forcing[0] + forcing[1]) + (forcing[2] + forcing[3]))
    rate = TIME_STEP * mobility
    trials = [jnp.clip(centre[a] + rate * (forcing[a] - mean), 0.0, 1.0) for a in range(PHASES)]
    scale = 1.0 / ((trials[0] + trials[1]) + (trials[2] + trials[3]))
    phases = [t * scale for t in trials]
    slope = 0.5 * TIME_STEP * (LIQUID_DIFFUSION - SOLID_DIFFUSION)
    base = 0.5 * TIME_STEP * 2.0 * SOLID_DIFFUSION
    own = slope * centre[0] + base
    inflow = [None, None]
    for side in (above, below, prev, after, left, right):
        both = slope * side[0] + own
        for k in range(SOLUTES):
            flux = both * (side[4 + k] - centre[4 + k])
            inflow[k] = flux if inflow[k] is None else inflow[k] + flux
    changes = [phases[a] - centre[a] for a in range(PHASES)]
    solutes = []
    for k in range(SOLUTES):
        rejected = (partition(k, 0) * changes[0] + partition(k, 1) * changes[1]) + (
            partition(k, 2) * changes[2] + partition(k, 3) * changes[3]
        )
        solutes.append(centre[4 + k] + (inflow[k] - rejected))
    return phases + solutes


class Rows:
    def __init__(self, plan, *groups):
        self.pitch = plan.pitch
        self.place = {}
        for ref, rows in groups:
            for slot, w in enumerate(rows):
                self.place[w] = (ref, slot * plan.pitch)

    def load(self, f, w, j, count=TILE):
        ref, base = self.place[w]
        return ref[f, pl.ds(base + j, count), :]

    def store(self, f, w, j, value):
        ref, base = self.place[w]
        ref[f, pl.ds(base + j, value.shape[0]), :] = value


def fill_cooling(plan, cooling, first):
    ramp = lax.broadcasted_iota(jnp.int32, (TILE, 128), 0)
    for j in range(0, plan.depth, TILE):
        height = (ramp + (first + j)).astype(F32)
        undercool = 2.0 * (0.5 - (height + 0.5) * (1.0 / plan.total))
        for a in range(PHASES):
            cooling[a, pl.ds(j, TILE), :] = COOLING_WEIGHTS[a] * undercool - 0.5


def sweep(w, j, source, mobility, cooling, partition):
    def load(f, dz, dr):
        return source.load(f, w + dr, j + dz)

    def rate(k, a):
        return partition[pl.ds((k * PHASES + a) * TILE, TILE), :]

    return step_tile(load, lambda a: cooling[a, pl.ds(j, TILE), :], mobility.load(0, w, j), rate)


def run_step(plan, step, rows, source, target, mobility, cooling, partition):
    for w in rows:
        for j in plan.starts(step, w):
            new = sweep(w, j, source, mobility, cooling, partition)
            for f in range(FIELDS):
                target.store(f, w, j, new[f])


def repeat_plane(fields, rows, source, target):
    for w in rows:
        for f in range(FIELDS):
            fields.store(f, w, target, fields.load(f, w, source, 1))


def fill_liquid(plan, fields, rows):
    count = plan.depth - 2 - plan.own
    for w in rows:
        for f in range(FIELDS):
            fields.store(f, w, plan.own, jnp.full((count, 128), INFLOW[f], F32))


def put_raw(fields, mobility, array, w, j, tile):
    if array == 0:
        for a in range(PHASES):
            fields.store(a, w, j, jnp.where(tile == a, 1.0, 0.0))
    elif array == 3:
        mobility.store(0, w, j, tile)
    else:
        fields.store(PHASES - 1 + array, w, j, tile)


def row_sets(plan):
    own = list(range(STEPS, STEPS + plan.rows))
    inner = [own[step:-step] for step in range(STEPS + 1)]
    outer = [
        [w for w in range(step, plan.wide - step) if w not in inner[step]] for step in range(STEPS + 1)
    ]
    inner[0] = own
    outer[0] = [w for w in range(plan.wide) if w not in own]
    return inner, outer


def inner_kernel(plan, own, grow, partition, f0, m0, f1, f2, f3, cooling, late_cooling):
    rows = plan.rows
    inner, _ = row_sets(plan)
    slab = lax.axis_index("grow")
    first_slab, last_slab = slab == 0, slab == plan.slabs - 1
    edge = plan.own - 1
    raw, mobility = Rows(plan, (f0, inner[0])), Rows(plan, (m0, inner[0]))
    once, twice, final = Rows(plan, (f1, inner[1])), Rows(plan, (f2, inner[2])), Rows(plan, (f3, inner[3]))
    fill_cooling(plan, cooling, slab * plan.planes + SHIFT - STEPS)
    fill_cooling(plan, late_cooling, slab * plan.planes - STEPS)

    for array in range(RAW):
        for source, begin, length in ((own, 0, plan.own), (grow, plan.own, plan.next)):
            for w in inner[0]:
                for k in range(0, length, TILE):
                    n = min(TILE, length - k)
                    at = (array * length + k) * rows + w - STEPS
                    put_raw(raw, mobility, array, w, begin + k, source[pl.ds(at, n, stride=rows), :])

    @pl.when(last_slab)
    def _():
        repeat_plane(raw, inner[0], edge, edge + 1)

    run_step(plan, 1, inner[1], raw, once, mobility, cooling, partition)

    @pl.when(last_slab)
    def _():
        repeat_plane(once, inner[1], edge, edge + 1)

    run_step(plan, 2, inner[2], once, twice, mobility, cooling, partition)

    @pl.when(last_slab)
    def _():
        fill_liquid(plan, twice, inner[2])
        count = plan.depth - 2 - plan.own
        for w in inner[0]:
            mobility.store(0, w, plan.own, jnp.full((count, 128), LIQUID_MOBILITY, F32))

    @pl.when(first_slab)
    def _():
        repeat_plane(twice, inner[2], STEPS, STEPS - 1)

    run_step(plan, 3, inner[3], twice, final, mobility, late_cooling, partition)


def outer_kernel(plan, f0, m0, f1, f2, f3, partition, *refs):
    n_own, n_next = len(plan.own_rows), len(plan.next_rows)
    own_halos, next_halos = refs[:n_own], refs[n_own : n_own + 2 * n_next]
    phase_out, solute_out, x0, xm, x1, x2, result, cooling, late_cooling, sems = refs[n_own + 2 * n_next :]
    rows = plan.rows
    inner, outer = row_sets(plan)
    slab = lax.axis_index("grow")
    first_slab, last_slab = slab == 0, slab == plan.slabs - 1
    odd = lax.rem(slab, 2) == 1
    edge = plan.own - 1
    raw = Rows(plan, (f0, inner[0]), (x0, outer[0]))
    mobility = Rows(plan, (m0, inner[0]), (xm, [w for w in outer[0] if plan.away(w) < STEPS]))
    once, twice = Rows(plan, (f1, inner[1]), (x1, outer[1])), Rows(plan, (f2, inner[2]), (x2, outer[2]))
    done = Rows(plan, (f3, inner[3]))
    fill_cooling(plan, cooling, slab * plan.planes + SHIFT - STEPS)
    fill_cooling(plan, late_cooling, slab * plan.planes - STEPS)

    for runs, buffers in ((plan.own_runs, own_halos), (plan.next_runs, next_halos)):
        for side, array, distance, j, count, buffer, offset in runs:
            w = STEPS + rows - 1 + distance if side == 0 else STEPS - distance
            for k in range(0, count, TILE):
                n = min(TILE, count - k)
                tile = buffers[buffer][pl.ds(offset + k, n), :]
                if len(buffers) > n_next:
                    tile = jnp.where(odd, buffers[buffer + n_next][pl.ds(offset + k, n), :], tile)
                put_raw(raw, mobility, array, w, j + k, tile)

    @pl.when(last_slab)
    def _():
        repeat_plane(raw, outer[0], edge, edge + 1)

    run_step(plan, 1, outer[1], raw, once, mobility, cooling, partition)

    @pl.when(last_slab)
    def _():
        repeat_plane(once, outer[1], edge, edge + 1)

    run_step(plan, 2, outer[2], once, twice, mobility, cooling, partition)

    @pl.when(last_slab)
    def _():
        fill_liquid(plan, twice, outer[2])

    @pl.when(first_slab)
    def _():
        repeat_plane(twice, outer[2], STEPS, STEPS - 1)

    copies = []
    sent = 0
    for j in plan.starts(3, STEPS):
        for w in inner[0]:
            if w in inner[3]:
                new = [done.load(f, w, j) for f in range(FIELDS)]
            else:
                new = sweep(w, j, twice, mobility, late_cooling, partition)
            for f in range(FIELDS):
                result[f, pl.ds((j - STEPS) * rows + w - STEPS, TILE, stride=rows), :] = new[f]
        ready = (j - STEPS + TILE) * rows
        part = pl.ds(sent, ready - sent)
        for out, begin, count in ((phase_out, 0, PHASES), (solute_out, PHASES, SOLUTES)):
            copies.append(
                pltpu.make_async_copy(
                    result.at[pl.ds(begin, count), part], out.at[:, part], sems.at[len(copies)]
                )
            )
            copies[-1].start()
        sent = ready
    for copy in copies:
        copy.wait()


def on_chip(value):
    return pltpu.with_memory_space_constraint(value, pltpu.VMEM)


def shards(phase_label, grain_label, grain_orient, orient_mobility, solute_init, partition):
    slabs, blocks = lax.axis_size("grow"), lax.axis_size("trans")
    planes, rows, columns = phase_label.shape
    plan = Plan(planes, rows, slabs, blocks)
    inner, outer = row_sets(plan)
    vmem, hbm = (pl.BlockSpec(memory_space=m) for m in (pltpu.VMEM, pltpu.HBM))

    def field_rows(count, fields=FIELDS):
        return pltpu.VMEM((fields, count * plan.pitch, columns), F32)

    halo_shapes = [pltpu.VMEM((length, columns), F32) for length in plan.own_rows + plan.next_rows]
    inputs = (phase_label, grain_label, solute_init, grain_orient, orient_mobility, partition.T)
    own, grow, rates, *halos = pl.pallas_call(
        functools.partial(pack_kernel, plan),
        out_shape=[
            pltpu.VMEM((RAW * plan.own * rows, columns), F32),
            pltpu.VMEM((RAW * plan.next * rows, columns), F32),
            pltpu.VMEM((SOLUTES * PHASES * TILE, columns), F32),
            *halo_shapes,
        ],
        in_specs=[hbm] * len(inputs),
        out_specs=[vmem] * (3 + len(halo_shapes)),
        scratch_shapes=[
            (pltpu.VMEM if value.ndim > 2 else pltpu.SMEM)(value.shape, value.dtype) for value in inputs
        ]
        + [pltpu.SemaphoreType.DMA((len(inputs),))],
        compiler_params=PARAMS,
        name="pack",
    )(*(pltpu.with_memory_space_constraint(value, pltpu.HBM) for value in inputs))

    ups = [(b + 1) % blocks for b in range(blocks)]
    downs = [(b - 1) % blocks for b in range(blocks)]

    def fetch(value, side, hop, targets, closed=True):
        others = ups if side == 0 else downs
        pairs = [(((s + hop) % slabs) * blocks + others[b], s * blocks + b) for s in targets for b in range(blocks)]
        if closed:
            senders, takers = ({pair[i] for pair in pairs} for i in range(2))
            idle = [
                [i for i in range(slabs * blocks) if i not in busy] for busy in (senders, takers)
            ]
            pairs += zip(*(sorted(i, key=lambda d: (d // blocks // 2, d % blocks)) for i in idle))
        return lax.ppermute(value, ("grow", "trans"), pairs)

    n_own = len(plan.own_rows)
    own_halos = [fetch(value, side, 0, range(slabs)) for side, value in enumerate(halos[:n_own])]
    even_halos = [fetch(v, side, 1, range(0, slabs - 1, 2)) for side, v in enumerate(halos[n_own:])]
    odd_halos = [fetch(v, side, 1, range(1, slabs - 1, 2), closed=False) for side, v in enumerate(halos[n_own:])]
    received = lax.ppermute(grow, "grow", [(s + 1, s) for s in range(slabs - 1)])
    cooling = pltpu.VMEM((PHASES, plan.pitch, columns), F32)
    state = pl.pallas_call(
        functools.partial(inner_kernel, plan),
        out_shape=[
            field_rows(len(inner[0])),
            field_rows(len(inner[0]), 1),
            field_rows(len(inner[1])),
            field_rows(len(inner[2])),
            field_rows(len(inner[3])),
        ],
        in_specs=[vmem] * 3,
        out_specs=[vmem] * 5,
        scratch_shapes=[cooling, cooling],
        cost_estimate=pl.CostEstimate(flops=8_000_000, bytes_accessed=0, transcendentals=0),
        compiler_params=PARAMS,
        name="inner",
    )(*(on_chip(x) for x in (own, received, rates)))
    halos = own_halos + even_halos + odd_halos
    phase_out, solute_out = pl.pallas_call(
        functools.partial(outer_kernel, plan),
        out_shape=[
            jax.ShapeDtypeStruct((PHASES, planes * rows, columns), F32),
            jax.ShapeDtypeStruct((SOLUTES, planes * rows, columns), F32),
        ],
        in_specs=[vmem] * (6 + len(halos)),
        out_specs=[hbm, hbm],
        scratch_shapes=[
            field_rows(len(outer[0])),
            field_rows(len(outer[0]) - 2, 1),
            field_rows(len(outer[1])),
            field_rows(len(outer[2])),
            pltpu.VMEM((FIELDS, planes * rows, columns), F32),
            cooling,
            cooling,
            pltpu.SemaphoreType.DMA((2 * len(plan.starts(3, STEPS)),)),
        ],
        cost_estimate=pl.CostEstimate(flops=8_000_000, bytes_accessed=0, transcendentals=0),
        compiler_params=PARAMS,
        name="outer",
    )(*(on_chip(x) for x in (*state, rates, *halos)))
    return (
        phase_out.reshape(PHASES, planes, rows, columns),
        solute_out.reshape(SOLUTES, planes, rows, columns),
    )


def solution(mesh):
    placed = (
        P("grow", "trans", None),
        P("grow", "trans", None),
        P(),
        P(),
        P(None, "grow", "trans", None),
        P(),
    )
    return jax.shard_map(
        shards,
        mesh=mesh,
        in_specs=placed,
        out_specs=(P(None, "grow", "trans", None), P(None, "grow", "trans", None)),
        check_vma=False,
    )
```

time: 21.1 us -> 20.2 us (0.957)
  the two profiles are of different devices: /device:TPU:9 before, /device:TPU:17 now
where the time goes in v3:
time: 20.2 us; the launch traced here: 20 us
  starting transfers between devices  8.35 us (41%)
  waiting for transfers between devices  5.91 us (29%)
  Pallas kernels  5.06 us (25%)
  between operations  0.66 us (3%)
    ppermute x3, waiting for transfers between devices, fetch(): return lax.ppermute(value, ('grow', 'trans'), pairs)  5.91 us
    ppermute x3, starting transfers between devices, fetch(): return lax.ppermute(value, ('grow', 'trans'), pairs)  5.77 us
    ppermute x1, starting transfers between devices, shards(): lax.ppermute(grow, 'grow', [(s + 1, s) for s in range(slabs - 1)])  2.58 us
    pallas_call x1, Pallas kernels, shards(): pl.pallas_call(functools.partial(outer_kernel, plan), out_shape=[jax.Shap...  2.42 us
    pallas_call x1, Pallas kernels, shards(): pl.pallas_call(functools.partial(inner_kernel, plan), out_shape=[field_ro...  1.35 us
    pallas_call x1, Pallas kernels, shards(): pl.pallas_call(functools.partial(pack_kernel, plan), out_shape=[pltpu.VME...  1.29 us
  transfers between devices with their start and end apart: 4, of which 1 were waited for; matrix products, arithmetic and copies ran while one was open for 0% of the time, Pallas kernels for 7%

profile of v3, /device:TPU:17, one launch (start us, length us, event | category | flops | bytes accessed | tf_op | source)
XLA Modules:
  0.0 20.0 jit_solution(13232174006787799674)
XLA Ops:
  0.6 1.3 %pack.1 = (f32[352,128]{1,0:T(8,128)S(1)}, f32[608,128]{1,0:T(8,128)S(1)}, f32[64,128]{1,0:T(8,128)S(1)}, f32[200,128]{1,0:T(8,128)S(1)}, f32[376,128]{1,0:T(8,128)S(1)}) custom-call(s32[24,8,128]{2,1,0:T(8,128)} %refs_0_.1, s32[24,8,128]{2,1,0:T(8,128)} %refs_1_.1, f32[2,24,8,128]{3,2,1,0:T(8,128)} %refs_2_.1, s32[32]{0:T(128)} %refs_3_.1, f32[8]{0:T(128)} %refs_4_.1, ...), custom_call_target="tpu_custom_call" | custom-call | tf_op jit(solution)/shard_map/pack/pallas_call | solution.py:365
  1.9 2.6 %collective-permute-start = (f32[608,128]{1,0:T(8,128)S(1)}, f32[608,128]{1,0:T(8,128)S(1)}, u32[]{:S(2)}, u32[]{:S(2)}) collective-permute-start(f32[608,128]{1,0:T(8,128)S(1)} %get-tuple-element.15), channel_id=1, source_target_pairs={{2,0},{4,2},{6,4},{8,6},{10,8},{12,10},{14,12},{16,14},{18,16},{20... | collective-permute-start | bytes 933896 | tf_op jit(solution)/shard_map/ppermute | solution.py:401
  4.5 1.3 %collective-permute-start.3 = (f32[376,128]{1,0:T(8,128)S(1)}, f32[376,128]{1,0:T(8,128)S(1)}, u32[]{:S(2)}, u32[]{:S(2)}) collective-permute-start(f32[376,128]{1,0:T(8,128)S(1)} %get-tuple-element.23), channel_id=1, source_target_pairs={{5,2},{4,3},{9,6},{8,7},{13,10},{12,11},{17,14},{16,15},{21,18},{2... | collective-permute-start | bytes 577544 | tf_op jit(solution)/shard_map/ppermute | solution.py:395
  5.8 3.3 %collective-permute-start.2 = (f32[376,128]{1,0:T(8,128)S(1)}, f32[376,128]{1,0:T(8,128)S(1)}, u32[]{:S(2)}, u32[]{:S(2)}) collective-permute-start(f32[376,128]{1,0:T(8,128)S(1)} %get-tuple-element.23), channel_id=1, source_target_pairs={{3,0},{2,1},{7,4},{6,5},{11,8},{10,9},{15,12},{14,13},{19,16},{18,... | collective-permute-start | bytes 577544 | tf_op jit(solution)/shard_map/ppermute | solution.py:395
  9.1 1.2 %collective-permute-start.1 = (f32[200,128]{1,0:T(8,128)S(1)}, f32[200,128]{1,0:T(8,128)S(1)}, u32[]{:S(2)}, u32[]{:S(2)}) collective-permute-start(f32[200,128]{1,0:T(8,128)S(1)} %get-tuple-element.22), channel_id=1, source_target_pairs={{1,0},{0,1},{3,2},{2,3},{5,4},{4,5},{7,6},{6,7},{9,8},{8,9},{11,10... | collective-permute-start | bytes 307208 | tf_op jit(solution)/shard_map/ppermute | solution.py:395
  10.3 0.0 collective-permute-done.grow
  10.3 1.4 %inner.1 = (f32[6,320,128]{2,1,0:T(8,128)S(1)}, f32[1,320,128]{2,1,0:T(8,128)S(1)}, f32[6,240,128]{2,1,0:T(8,128)S(1)}, f32[6,160,128]{2,1,0:T(8,128)S(1)}, f32[6,80,128]{2,1,0:T(8,128)S(1)}) custom-call(f32[352,128]{1,0:T(8,128)S(1)} %get-tuple-element.14.own, f32[608,128]{1,0:T(8,128)S(1)} %collective-permute-done.grow, ...), custom_call_target="tpu_custom_call" | custom-call | flops 8000000 | tf_op jit(solution)/shard_map/inner/pallas_call | solution.py:403
  11.7 5.9 %collective-permute-done.1.refs_0_ = f32[200,128]{1,0:T(8,128)S(1)} collective-permute-done((f32[200,128]{1,0:T(8,128)S(1)}, f32[200,128]{1,0:T(8,128)S(1)}, u32[]{:S(2)}, u32[]{:S(2)}) %collective-permute-start.1) | collective-permute-done | bytes 102432 | tf_op jit(solution)/shard_map/ppermute | solution.py:395
  17.6 0.0 collective-permute-done.3.refs_2_
  17.6 0.0 collective-permute-done.2.refs_1_
  17.6 2.4 %outer.1 = (f32[4,192,128]{2,1,0:T(8,128)}, f32[2,192,128]{2,1,0:T(8,128)}) custom-call(f32[6,320,128]{2,1,0:T(8,128)S(1)} %get-tuple-element.17.f0, f32[1,320,128]{2,1,0:T(8,128)S(1)} %get-tuple-element.18.m0, f32[6,240,128]{2,1,0:T(8,128)S(1)} %get-tuple-element.19.f1, f32[6,160,128]{2,1,0:T(8,128)S(1)} %get-tuple-element.20.f2, ...), custom_call_target="tpu_custom_call" | custom-call | flops 8000000 | tf_op jit(solution)/shard_map/outer/pallas_call | solution.py:420
Async XLA Ops:
  1.9 8.4 %collective-permute-start = (f32[608,128]{1,0:T(8,128)S(1)}, f32[608,128]{1,0:T(8,128)S(1)}, u32[]{:S(2)}, u32[]{:S(2)}) collective-permute-start(f32[608,128]{1,0:T(8,128)S(1)} %get-tuple-element.15), channel_id=1, source_target_pairs={{2,0},{4,2},{6,4},{8,6},{10,8},{12,10},{14,12},{16,14},{18,16},{20... | collective-permute-start | bytes 933896 | tf_op jit(solution)/shard_map/ppermute | solution.py:401
  4.5 13.0 %collective-permute-start.3 = (f32[376,128]{1,0:T(8,128)S(1)}, f32[376,128]{1,0:T(8,128)S(1)}, u32[]{:S(2)}, u32[]{:S(2)}) collective-permute-start(f32[376,128]{1,0:T(8,128)S(1)} %get-tuple-element.23), channel_id=1, source_target_pairs={{5,2},{4,3},{9,6},{8,7},{13,10},{12,11},{17,14},{16,15},{21,18},{2... | collective-permute-start | bytes 577544 | tf_op jit(solution)/shard_map/ppermute | solution.py:395
  5.8 11.7 %collective-permute-start.2 = (f32[376,128]{1,0:T(8,128)S(1)}, f32[376,128]{1,0:T(8,128)S(1)}, u32[]{:S(2)}, u32[]{:S(2)}) collective-permute-start(f32[376,128]{1,0:T(8,128)S(1)} %get-tuple-element.23), channel_id=1, source_target_pairs={{3,0},{2,1},{7,4},{6,5},{11,8},{10,9},{15,12},{14,13},{19,16},{18,... | collective-permute-start | bytes 577544 | tf_op jit(solution)/shard_map/ppermute | solution.py:395
  9.1 8.5 %collective-permute-start.1 = (f32[200,128]{1,0:T(8,128)S(1)}, f32[200,128]{1,0:T(8,128)S(1)}, u32[]{:S(2)}, u32[]{:S(2)}) collective-permute-start(f32[200,128]{1,0:T(8,128)S(1)} %get-tuple-element.22), channel_id=1, source_target_pairs={{1,0},{0,1},{3,2},{2,3},{5,4},{4,5},{7,6},{6,7},{9,8},{8,9},{11,10... | collective-permute-start | bytes 307208 | tf_op jit(solution)/shard_map/ppermute | solution.py:395

commit v4 on v3

--- a/solution.py
+++ b/solution.py
@@ -14,6 +14,7 @@
 PHASES = 4
 SOLUTES = 2
 FIELDS = PHASES + SOLUTES
+STORED = FIELDS + SOLUTES
 RAW = 4
 TILE = 8
 
@@ -27,6 +28,9 @@
 SECOND_WEIGHTS = (0.4, 0.3, -1.0, 0.5)
 INFLOW = (1.0, 0.0, 0.0, 0.0, 0.3, 0.2)
 LIQUID_MOBILITY = 1.0
+SLOPE = 0.5 * TIME_STEP * (LIQUID_DIFFUSION - SOLID_DIFFUSION)
+BASE = 0.5 * TIME_STEP * 2.0 * SOLID_DIFFUSION
+INFLOW = INFLOW + (SLOPE * INFLOW[0] * INFLOW[4], SLOPE * INFLOW[0] * INFLOW[5])
 
 F32 = jnp.float32
 PARAMS = pltpu.CompilerParams(vmem_limit_bytes=16 * 1024 * 1024)
@@ -37,8 +41,8 @@
 
 
 class Plan:
-    def __init__(self, planes, rows, slabs, blocks):
-        self.planes, self.rows, self.slabs, self.blocks = planes, rows, slabs, blocks
+    def __init__(self, planes, rows, columns, slabs, blocks):
+        self.planes, self.rows, self.columns, self.slabs, self.blocks = planes, rows, columns, slabs, blocks
         self.own = planes - SHIFT + STEPS
         self.next = SHIFT + STEPS
         self.depth = self.own + self.next
@@ -84,11 +88,11 @@
     rows = plan.rows
     for k in range(SOLUTES):
         for a in range(PHASES):
-            rates[pl.ds((k * PHASES + a) * TILE, TILE), :] = jnp.full((TILE, 128), partition[k, a])
-    table = jnp.zeros((rows, 128), F32)
-    lanes = lax.broadcasted_iota(jnp.int32, (rows, 128), 1)
+            rates[pl.ds((k * PHASES + a) * TILE, TILE), :] = jnp.full((TILE, plan.columns), partition[k, a])
+    table = jnp.zeros((rows, plan.columns), F32)
+    lanes = lax.broadcasted_iota(jnp.int32, (rows, plan.columns), 1)
     for g in range(orient.shape[0]):
-        table = jnp.where(lanes == g, mobil[orient[g]], table)
+        table = jnp.where(lanes == g, TIME_STEP * mobil[orient[g]], table)
     first = SHIFT - STEPS
     for z in range(plan.planes):
         label = phase[z].astype(F32)
@@ -111,44 +115,35 @@
                 buffers[buffer][pl.ds(offset + k, n), :] = source[pl.ds(at, n, stride=rows), :]
 
 
-def step_tile(load, cooling, mobility, partition):
-    centre = [load(f, 0, 0) for f in range(FIELDS)]
-    below = [load(f, -1, 0) for f in range(FIELDS)]
-    above = [load(f, 1, 0) for f in range(FIELDS)]
-    prev = [load(f, 0, -1) for f in range(FIELDS)]
-    after = [load(f, 0, 1) for f in range(FIELDS)]
-    left = [pltpu.roll(c, 1, 1) for c in centre]
-    right = [pltpu.roll(c, c.shape[1] - 1, 1) for c in centre]
+def step_tile(load, cooling, rate, partition):
+    centre = [load(f, 0, 0) for f in range(STORED)]
+    depth, flat = [], []
+    for f in range(STORED):
+        depth.append(load(f, 1, 0) + load(f, -1, 0))
+        turned = pltpu.roll(centre[f], 1, 1) + pltpu.roll(centre[f], centre[f].shape[1] - 1, 1)
+        flat.append((load(f, 0, -1) + load(f, 0, 1)) + turned)
     c0, c1 = centre[4], centre[5]
     forcing = []
     for a in range(PHASES):
         p = centre[a]
-        laplace = ANISOTROPY * (above[a] + below[a]) + ((prev[a] + after[a]) + (left[a] + right[a]))
-        laplace = laplace - (2.0 * ANISOTROPY + 4.0) * p
-        driving = cooling(a) + FIRST_WEIGHTS[a] * c0 + SECOND_WEIGHTS[a] * c1
-        well = WELL_HEIGHT * p
-        forcing.append(laplace + (well - well * p) * (p + driving))
+        driving = cooling(a) + (WELL_HEIGHT * FIRST_WEIGHTS[a]) * c0 + (WELL_HEIGHT * SECOND_WEIGHTS[a]) * c1
+        well = (1.0 - p) * (WELL_HEIGHT * p + driving) - (2.0 * ANISOTROPY + 4.0)
+        forcing.append((ANISOTROPY * depth[a] + flat[a]) + p * well)
     mean = 0.25 * ((forcing[0] + forcing[1]) + (forcing[2] + forcing[3]))
-    rate = TIME_STEP * mobility
     trials = [jnp.clip(centre[a] + rate * (forcing[a] - mean), 0.0, 1.0) for a in range(PHASES)]
     scale = 1.0 / ((trials[0] + trials[1]) + (trials[2] + trials[3]))
     phases = [t * scale for t in trials]
-    slope = 0.5 * TIME_STEP * (LIQUID_DIFFUSION - SOLID_DIFFUSION)
-    base = 0.5 * TIME_STEP * 2.0 * SOLID_DIFFUSION
-    own = slope * centre[0] + base
-    inflow = [None, None]
-    for side in (above, below, prev, after, left, right):
-        both = slope * side[0] + own
-        for k in range(SOLUTES):
-            flux = both * (side[4 + k] - centre[4 + k])
-            inflow[k] = flux if inflow[k] is None else inflow[k] + flux
+    own = SLOPE * centre[0] + BASE
+    outflow = SLOPE * (depth[0] + flat[0]) + 6.0 * own
     changes = [phases[a] - centre[a] for a in range(PHASES)]
     solutes = []
     for k in range(SOLUTES):
+        c, product = 4 + k, FIELDS + k
+        inflow = (depth[product] + flat[product]) + own * (depth[c] + flat[c]) - outflow * centre[c]
         rejected = (partition(k, 0) * changes[0] + partition(k, 1) * changes[1]) + (
             partition(k, 2) * changes[2] + partition(k, 3) * changes[3]
         )
-        solutes.append(centre[4 + k] + (inflow[k] - rejected))
+        solutes.append(centre[c] + (inflow - rejected))
     return phases + solutes
 
 
@@ -170,12 +165,12 @@
 
 
 def fill_cooling(plan, cooling, first):
-    ramp = lax.broadcasted_iota(jnp.int32, (TILE, 128), 0)
+    ramp = lax.broadcasted_iota(jnp.int32, (TILE, plan.columns), 0)
     for j in range(0, plan.depth, TILE):
         height = (ramp + (first + j)).astype(F32)
         undercool = 2.0 * (0.5 - (height + 0.5) * (1.0 / plan.total))
         for a in range(PHASES):
-            cooling[a, pl.ds(j, TILE), :] = COOLING_WEIGHTS[a] * undercool - 0.5
+            cooling[a, pl.ds(j, TILE), :] = WELL_HEIGHT * (COOLING_WEIGHTS[a] * undercool - 0.5)
 
 
 def sweep(w, j, source, mobility, cooling, partition):
@@ -192,21 +187,22 @@
     for w in rows:
         for j in plan.starts(step, w):
             new = sweep(w, j, source, mobility, cooling, partition)
-            for f in range(FIELDS):
-                target.store(f, w, j, new[f])
+            liquid = SLOPE * new[0]
+            for f, value in enumerate(new + [liquid * c for c in new[PHASES:]]):
+                target.store(f, w, j, value)
 
 
 def repeat_plane(fields, rows, source, target):
     for w in rows:
-        for f in range(FIELDS):
+        for f in range(STORED):
             fields.store(f, w, target, fields.load(f, w, source, 1))
 
 
 def fill_liquid(plan, fields, rows):
     count = plan.depth - 2 - plan.own
     for w in rows:
-        for f in range(FIELDS):
-            fields.store(f, w, plan.own, jnp.full((count, 128), INFLOW[f], F32))
+        for f in range(STORED):
+            fields.store(f, w, plan.own, jnp.full((count, plan.columns), INFLOW[f], F32))
 
 
 def put_raw(fields, mobility, array, w, j, tile):
@@ -217,6 +213,7 @@
         mobility.store(0, w, j, tile)
     else:
         fields.store(PHASES - 1 + array, w, j, tile)
+        fields.store(FIELDS - 1 + array, w, j, SLOPE * fields.load(0, w, j, tile.shape[0]) * tile)
 
 
 def row_sets(plan):
@@ -266,13 +263,17 @@
         fill_liquid(plan, twice, inner[2])
         count = plan.depth - 2 - plan.own
         for w in inner[0]:
-            mobility.store(0, w, plan.own, jnp.full((count, 128), LIQUID_MOBILITY, F32))
+            mobility.store(0, w, plan.own, jnp.full((count, plan.columns), TIME_STEP * LIQUID_MOBILITY, F32))
 
     @pl.when(first_slab)
     def _():
         repeat_plane(twice, inner[2], STEPS, STEPS - 1)
 
-    run_step(plan, 3, inner[3], twice, final, mobility, late_cooling, partition)
+    for w in inner[3]:
+        for j in plan.starts(3, w):
+            new = sweep(w, j, twice, mobility, late_cooling, partition)
+            for f in range(FIELDS):
+                final.store(f, w, j, new[f])
 
 
 def outer_kernel(plan, f0, m0, f1, f2, f3, partition, *refs):
@@ -353,11 +354,11 @@
 def shards(phase_label, grain_label, grain_orient, orient_mobility, solute_init, partition):
     slabs, blocks = lax.axis_size("grow"), lax.axis_size("trans")
     planes, rows, columns = phase_label.shape
-    plan = Plan(planes, rows, slabs, blocks)
+    plan = Plan(planes, rows, columns, slabs, blocks)
     inner, outer = row_sets(plan)
     vmem, hbm = (pl.BlockSpec(memory_space=m) for m in (pltpu.VMEM, pltpu.HBM))
 
-    def field_rows(count, fields=FIELDS):
+    def field_rows(count, fields=STORED):
         return pltpu.VMEM((fields, count * plan.pitch, columns), F32)
 
     halo_shapes = [pltpu.VMEM((length, columns), F32) for length in plan.own_rows + plan.next_rows]
@@ -385,7 +386,11 @@
 
     def fetch(value, side, hop, targets, closed=True):
         others = ups if side == 0 else downs
-        pairs = [(((s + hop) % slabs) * blocks + others[b], s * blocks + b) for s in targets for b in range(blocks)]
+        pairs = [
+            ((s + hop) * blocks + others[b] if s + hop < slabs else b, s * blocks + b)
+            for s in targets
+            for b in range(blocks)
+        ]
         if closed:
             senders, takers = ({pair[i] for pair in pairs} for i in range(2))
             idle = [
@@ -397,7 +402,7 @@
     n_own = len(plan.own_rows)
     own_halos = [fetch(value, side, 0, range(slabs)) for side, value in enumerate(halos[:n_own])]
     even_halos = [fetch(v, side, 1, range(0, slabs - 1, 2)) for side, v in enumerate(halos[n_own:])]
-    odd_halos = [fetch(v, side, 1, range(1, slabs - 1, 2), closed=False) for side, v in enumerate(halos[n_own:])]
+    odd_halos = [fetch(v, side, 1, range(1, slabs, 2)) for side, v in enumerate(halos[n_own:])]
     received = lax.ppermute(grow, "grow", [(s + 1, s) for s in range(slabs - 1)])
     cooling = pltpu.VMEM((PHASES, plan.pitch, columns), F32)
     state = pl.pallas_call(
@@ -407,7 +412,7 @@
             field_rows(len(inner[0]), 1),
             field_rows(len(inner[1])),
             field_rows(len(inner[2])),
-            field_rows(len(inner[3])),
+            field_rows(len(inner[3]), FIELDS),
         ],
         in_specs=[vmem] * 3,
         out_specs=[vmem] * 5,

time: 20.2 us -> 21.2 us (1.050)
  the two profiles are of different devices: /device:TPU:17 before, /device:TPU:1 now
where the time goes in v4:
time: 21.2 us; the launch traced here: 21.1 us
  starting transfers between devices  9.48 us (45%)
  waiting for transfers between devices  5.93 us (28%)
  Pallas kernels  5 us (24%)
  between operations  0.67 us (3%)
    ppermute x3, starting transfers between devices, fetch(): return lax.ppermute(value, ('grow', 'trans'), pairs)  7.56 us
    ppermute x3, waiting for transfers between devices, fetch(): return lax.ppermute(value, ('grow', 'trans'), pairs)  3.97 us
    pallas_call x1, Pallas kernels, shards(): pl.pallas_call(functools.partial(outer_kernel, plan), out_shape=[jax.Shap...  2.36 us
    ppermute x1, waiting for transfers between devices, shards(): lax.ppermute(grow, 'grow', [(s + 1, s) for s in range(slabs - 1)])  1.96 us
    ppermute x1, starting transfers between devices, shards(): lax.ppermute(grow, 'grow', [(s + 1, s) for s in range(slabs - 1)])  1.93 us
    pallas_call x1, Pallas kernels, shards(): pl.pallas_call(functools.partial(inner_kernel, plan), out_shape=[field_ro...  1.34 us
    pallas_call x1, Pallas kernels, shards(): pl.pallas_call(functools.partial(pack_kernel, plan), out_shape=[pltpu.VME...  1.3 us
  transfers between devices with their start and end apart: 4, of which 2 were waited for; matrix products, arithmetic and copies ran while one was open for 0% of the time, Pallas kernels for 6%

profile of v4, /device:TPU:1, one launch (start us, length us, event | category | flops | bytes accessed | tf_op | source)
XLA Modules:
  0.0 21.1 jit_solution(3835797410576158045)
XLA Ops:
  0.6 1.3 %pack.1 = (f32[352,128]{1,0:T(8,128)S(1)}, f32[608,128]{1,0:T(8,128)S(1)}, f32[64,128]{1,0:T(8,128)S(1)}, f32[200,128]{1,0:T(8,128)S(1)}, f32[376,128]{1,0:T(8,128)S(1)}) custom-call(s32[24,8,128]{2,1,0:T(8,128)} %refs_0_.1, s32[24,8,128]{2,1,0:T(8,128)} %refs_1_.1, f32[2,24,8,128]{3,2,1,0:T(8,128)} %refs_2_.1, s32[32]{0:T(128)} %refs_3_.1, f32[8]{0:T(128)} %refs_4_.1, ...), custom_call_target="tpu_custom_call" | custom-call | tf_op jit(solution)/shard_map/pack/pallas_call | solution.py:366
  1.9 1.9 %collective-permute-start = (f32[608,128]{1,0:T(8,128)S(1)}, f32[608,128]{1,0:T(8,128)S(1)}, u32[]{:S(2)}, u32[]{:S(2)}) collective-permute-start(f32[608,128]{1,0:T(8,128)S(1)} %get-tuple-element.15), channel_id=1, source_target_pairs={{2,0},{4,2},{6,4},{8,6},{10,8},{12,10},{14,12},{16,14},{18,16},{20... | collective-permute-start | bytes 933896 | tf_op jit(solution)/shard_map/ppermute | solution.py:406
  3.9 0.1 collective-permute-start.3
  3.9 7.2 %collective-permute-start.2 = (f32[376,128]{1,0:T(8,128)S(1)}, f32[376,128]{1,0:T(8,128)S(1)}, u32[]{:S(2)}, u32[]{:S(2)}) collective-permute-start(f32[376,128]{1,0:T(8,128)S(1)} %get-tuple-element.23), channel_id=1, source_target_pairs={{3,0},{2,1},{7,4},{6,5},{11,8},{10,9},{15,12},{14,13},{19,16},{18,... | collective-permute-start | bytes 577544 | tf_op jit(solution)/shard_map/ppermute | solution.py:400
  11.2 0.3 %collective-permute-start.1 = (f32[200,128]{1,0:T(8,128)S(1)}, f32[200,128]{1,0:T(8,128)S(1)}, u32[]{:S(2)}, u32[]{:S(2)}) collective-permute-start(f32[200,128]{1,0:T(8,128)S(1)} %get-tuple-element.22), channel_id=1, source_target_pairs={{1,0},{0,1},{3,2},{2,3},{5,4},{4,5},{7,6},{6,7},{9,8},{8,9},{11,10... | collective-permute-start | bytes 307208 | tf_op jit(solution)/shard_map/ppermute | solution.py:400
  11.4 2.0 %collective-permute-done.grow = f32[608,128]{1,0:T(8,128)S(1)} collective-permute-done((f32[608,128]{1,0:T(8,128)S(1)}, f32[608,128]{1,0:T(8,128)S(1)}, u32[]{:S(2)}, u32[]{:S(2)}) %collective-permute-start) | collective-permute-done | bytes 311328 | tf_op jit(solution)/shard_map/ppermute | solution.py:406
  13.4 1.3 %inner.1 = (f32[8,320,128]{2,1,0:T(8,128)S(1)}, f32[1,320,128]{2,1,0:T(8,128)S(1)}, f32[8,240,128]{2,1,0:T(8,128)S(1)}, f32[8,160,128]{2,1,0:T(8,128)S(1)}, f32[6,80,128]{2,1,0:T(8,128)S(1)}) custom-call(f32[352,128]{1,0:T(8,128)S(1)} %get-tuple-element.14.own, f32[608,128]{1,0:T(8,128)S(1)} %collective-permute-done.grow, ...), custom_call_target="tpu_custom_call" | custom-call | flops 8000000 | tf_op jit(solution)/shard_map/inner/pallas_call | solution.py:408
  14.7 4.0 %collective-permute-done.1.refs_0_ = f32[200,128]{1,0:T(8,128)S(1)} collective-permute-done((f32[200,128]{1,0:T(8,128)S(1)}, f32[200,128]{1,0:T(8,128)S(1)}, u32[]{:S(2)}, u32[]{:S(2)}) %collective-permute-start.1) | collective-permute-done | bytes 102432 | tf_op jit(solution)/shard_map/ppermute | solution.py:400
  18.7 0.0 collective-permute-done.3.refs_2_
  18.7 0.0 collective-permute-done.2.refs_1_
  18.7 2.4 %outer.1 = (f32[4,192,128]{2,1,0:T(8,128)}, f32[2,192,128]{2,1,0:T(8,128)}) custom-call(f32[8,320,128]{2,1,0:T(8,128)S(1)} %get-tuple-element.17.f0, f32[1,320,128]{2,1,0:T(8,128)S(1)} %get-tuple-element.18.m0, f32[8,240,128]{2,1,0:T(8,128)S(1)} %get-tuple-element.19.f1, f32[8,160,128]{2,1,0:T(8,128)S(1)} %get-tuple-element.20.f2, ...), custom_call_target="tpu_custom_call" | custom-call | flops 8000000 | tf_op jit(solution)/shard_map/outer/pallas_call | solution.py:425
Async XLA Ops:
  1.9 11.5 %collective-permute-start = (f32[608,128]{1,0:T(8,128)S(1)}, f32[608,128]{1,0:T(8,128)S(1)}, u32[]{:S(2)}, u32[]{:S(2)}) collective-permute-start(f32[608,128]{1,0:T(8,128)S(1)} %get-tuple-element.15), channel_id=1, source_target_pairs={{2,0},{4,2},{6,4},{8,6},{10,8},{12,10},{14,12},{16,14},{18,16},{20... | collective-permute-start | bytes 933896 | tf_op jit(solution)/shard_map/ppermute | solution.py:406
  3.9 14.8 %collective-permute-start.3 = (f32[376,128]{1,0:T(8,128)S(1)}, f32[376,128]{1,0:T(8,128)S(1)}, u32[]{:S(2)}, u32[]{:S(2)}) collective-permute-start(f32[376,128]{1,0:T(8,128)S(1)} %get-tuple-element.23), channel_id=1, source_target_pairs={{5,2},{4,3},{9,6},{8,7},{13,10},{12,11},{17,14},{16,15},{21,18},{2... | collective-permute-start | bytes 577544 | tf_op jit(solution)/shard_map/ppermute | solution.py:400
  3.9 14.8 %collective-permute-start.2 = (f32[376,128]{1,0:T(8,128)S(1)}, f32[376,128]{1,0:T(8,128)S(1)}, u32[]{:S(2)}, u32[]{:S(2)}) collective-permute-start(f32[376,128]{1,0:T(8,128)S(1)} %get-tuple-element.23), channel_id=1, source_target_pairs={{3,0},{2,1},{7,4},{6,5},{11,8},{10,9},{15,12},{14,13},{19,16},{18,... | collective-permute-start | bytes 577544 | tf_op jit(solution)/shard_map/ppermute | solution.py:400
  11.2 7.5 %collective-permute-start.1 = (f32[200,128]{1,0:T(8,128)S(1)}, f32[200,128]{1,0:T(8,128)S(1)}, u32[]{:S(2)}, u32[]{:S(2)}) collective-permute-start(f32[200,128]{1,0:T(8,128)S(1)} %get-tuple-element.22), channel_id=1, source_target_pairs={{1,0},{0,1},{3,2},{2,3},{5,4},{4,5},{7,6},{6,7},{9,8},{8,9},{11,10... | collective-permute-start | bytes 307208 | tf_op jit(solution)/shard_map/ppermute | solution.py:400
